TPU v7x, 128 devices: a whole 4x4x4 slice. The times are simulated.
128 devices in a mesh: edp: 2 (over z_lo), ep: 64 (over z_hi, x, y, core).
Axes of the slice: x: 4, y: 4, z: 4 (z_hi: 2, z_lo: 2; z = z_hi * 2 + z_lo), core: 2. Of those that a mesh axis runs over, the one named last changes fastest.
Arguments:
- tokens: bfloat16 [16384, 3584], P(('edp', 'ep')), may hold values from -6 to 6
- node_ids: int32 [16384, 4], P(('edp', 'ep')), may hold values from 0 to 7, as said below
- local_ids: int32 [16384, 8], P(('edp', 'ep')), may hold values from 0 to 15, as said below
- affinity: float32 [16384, 8], P(('edp', 'ep')), may hold values from 0.2 to 1
- w_gate: bfloat16 [128, 3584, 1024], P(('edp', 'ep')), may hold values from -0.09375 to 0.09375
- w_up: bfloat16 [128, 3584, 1024], P(('edp', 'ep')), may hold values from -0.09375 to 0.09375
- w_down: bfloat16 [128, 1024, 3584], P(('edp', 'ep')), may hold values from -0.1875 to 0.1875
- grad_parts: float32 [128, 3584, 128], P(('edp', 'ep')), may hold values from -2.5 to 2.5
Outputs:
- mixed: bfloat16 [16384, 3584], P(('edp', 'ep'))
- router_grad: float32 [3584, 128], P(('edp', 'ep'))
Inputs may be any that keep to these rules, and one draw needn't show every extreme that they name: `node_ids`: A token's 4 nodes are distinct and increasing. `local_ids`: columns 2 j and 2 j + 1 name the two experts 2 m and 2 m + 1 of one pair m of node node_ids[t, j], in either order. From the 128 tokens of one device each expert receives at most 10 routes; inside a node the loads from one device differ by at most one.
All inputs are finite; a program needn't handle non-finite values.
Results may differ from a plain program's by a relative error of at most 0.0057.
Values may be sent and summed in bfloat16 or wider, within the bound.
No kernel may reach another device: no remote copies, remote signals or barrier semaphores. Data moves between devices by JAX's collectives and lax.ppermute only.
A program may use at most 192 MiB of HBM per device.

v0:
```python
import functools

import jax
import jax.numpy as jnp
from jax import lax
from jax.experimental import pallas as pl
from jax.experimental.pallas import tpu as pltpu
from jax.sharding import Mesh, PartitionSpec as P


PAIRS, SLOTS, WIDE = 64, 5, 28
COEF_AT = SLOTS * WIDE
MSG = COEF_AT + 4
GRAD = 32
PITCH = MSG + 8
ROWS = PAIRS * SLOTS
CUTS = tuple(slice(16 * i, 16 * (i + 1)) for i in range(PAIRS // 16))
F32, BF16, I32 = jnp.float32, jnp.bfloat16, jnp.int32


def iota(shape, dim):
    return lax.broadcasted_iota(I32, shape, dim)


def pair_of(node_ref, local_ref, column):
    return node_ref[column : column + 1, :] * 8 + local_ref[2 * column : 2 * column + 1, :] // 2


def picks(node_ref, local_ref, start):
    tok = node_ref.shape[1]
    pair = iota((PAIRS, tok), 0)
    hit = jnp.zeros((PAIRS, tok), jnp.bool_)
    for column in range(4):
        hit = hit | (pair == pair_of(node_ref, local_ref, column))
    earlier = (iota((tok, tok), 0) < iota((tok, tok), 1)).astype(BF16)
    rank = jnp.dot(hit.astype(F32).astype(BF16), earlier, preferred_element_type=F32)
    return [jnp.where(hit & (rank == float(start + slot)), 1.0, 0.0) for slot in range(SLOTS)]


def lane_tile(j):
    return slice(128 * j, 128 * (j + 1))


def load_all(pairs, sem):
    copies = [pltpu.make_async_copy(src, dst, sem.at[i]) for i, (src, dst) in enumerate(pairs)]
    for copy in copies:
        copy.start()
    return copies


def send_kernel(start, node_in, local_in, aff_in, tok_in, *refs):
    grad_refs, (out_ref, flat_ref, stage_ref, node_ref, local_ref, aff_ref, tok_ref, sem) = refs[:-8], refs[-8:]
    here = ((node_in, node_ref), (local_in, local_ref), (aff_in, aff_ref), (tok_in, tok_ref))
    copies = load_all(here, sem)
    for copy in copies[:3]:
        copy.wait()
    each = picks(node_ref, local_ref, start)
    pick = jnp.concatenate(each, axis=0).astype(BF16)
    copies[3].wait()
    for k in range(7):
        rows = jnp.dot(pick, tok_ref[:, 512 * k : 512 * (k + 1)], preferred_element_type=F32)
        for m in range(4):
            for s in range(SLOTS):
                at = pl.ds(s * WIDE + 4 * k + m, PAIRS, stride=PITCH)
                flat_ref[at, :] = rows[PAIRS * s : PAIRS * (s + 1), lane_tile(m)]
    aff = aff_ref[...]
    weight = 2.5 * aff / jnp.sum(aff, axis=0, keepdims=True)
    tok = node_ref.shape[1]
    pair = iota((PAIRS, tok), 0)
    even = jnp.zeros((PAIRS, tok), F32)
    odd = jnp.zeros((PAIRS, tok), F32)
    for column in range(4):
        first, second = weight[2 * column : 2 * column + 1, :], weight[2 * column + 1 : 2 * column + 2, :]
        flip = local_ref[2 * column : 2 * column + 1, :] % 2 == 1
        here = pair == pair_of(node_ref, local_ref, column)
        even = jnp.where(here, jnp.where(flip, second, first), even)
        odd = jnp.where(here, jnp.where(flip, first, second), odd)
    lane = iota((PAIRS, 128), 1)
    coef = jnp.zeros((PAIRS, 128), F32)
    for slot in range(SLOTS):
        even_w = jnp.sum(each[slot] * even, axis=1, keepdims=True)
        odd_w = jnp.sum(each[slot] * odd, axis=1, keepdims=True)
        coef = jnp.where(lane // 2 == 2 * slot, even_w, coef)
        coef = jnp.where(lane // 2 == 2 * slot + 1, odd_w, coef)
    high = coef.astype(BF16).astype(F32)
    coef = jnp.where(lane % 2 == 0, high, coef - high)
    for row in range(COEF_AT, MSG):
        flat_ref[pl.ds(row, PAIRS, stride=PITCH), :] = coef
    saves = []
    for i, cut in enumerate(CUTS):
        stage_ref[cut, :MSG, :] = flat_ref.reshape(PAIRS, PITCH, 128)[cut, :MSG, :].astype(BF16)
        if grad_refs:
            keep_ref, got_ref = grad_refs
            stage_ref[cut, MSG:, :] = (keep_ref[cut] + got_ref[cut].astype(F32)).astype(BF16)
        saves.append(pltpu.make_async_copy(stage_ref.at[cut], out_ref.at[cut], sem.at[4 + i]))
        saves[-1].start()
    for save in saves:
        save.wait()


def halves_kernel(core_ref, in_ref, keep_ref, give_ref):
    blocks = in_ref.reshape(PAIRS, 2 * WIDE, 128)
    first = core_ref[0] == 0
    low, high = blocks[:, :24, :], blocks[:, 32:, :]
    shared = blocks[:, 24:32, :]
    keep_ref[:, :24, :] = jnp.where(first, low, high)
    keep_ref[:, 24:, :] = shared
    give_ref[:, :24, :] = jnp.where(first, high, low).astype(BF16)
    give_ref[:, 24:, :] = shared.astype(BF16)


def spread(src_ref, flat_ref):
    flat_ref.reshape(PAIRS, PITCH, 128)[:, :MSG, :] = src_ref[:, :MSG, :].astype(F32)


def lay_out(flat_ref, rows_ref, first, last):
    for s in range(SLOTS):
        for j in range(first, last):
            tile = flat_ref[pl.ds(s * WIDE + j, PAIRS, stride=PITCH), :]
            rows_ref[PAIRS * s : PAIRS * (s + 1), lane_tile(j)] = tile.astype(BF16)


PIECE, PIECES = 512, 7


def expert_kernel(
    core_ref, in_ref, gate_ref, up_ref, down_ref, out_ref,
    flat, rows, gate, up, down, acc, hid, w_ref, sem_g, sem_u, sem_d,
):
    hidden = gate.shape[1]

    def cut(k):
        return pl.ds(pl.multiple_of(k * PIECE, PIECE), PIECE)

    def gate_copy(k):
        return pltpu.make_async_copy(gate_ref.at[0, cut(k), :], gate.at[cut(k), :], sem_g.at[k])

    def up_copy(k):
        return pltpu.make_async_copy(up_ref.at[0, cut(k), :], up.at[cut(k), :], sem_u.at[k])

    down_copy = pltpu.make_async_copy(down_ref.at[0], down, sem_d.at[0])
    for k in range(3):
        gate_copy(k).start()
        up_copy(k).start()
    spread(in_ref, flat)
    core = core_ref[0]
    coef = flat[pl.ds(COEF_AT, PAIRS, stride=PITCH), :]
    lane = iota((PAIRS, 128), 1)
    for s in range(SLOTS):
        mine = jnp.where(lane // 2 == 2 * s + core, coef, 0.0)
        w_ref[PAIRS * s : PAIRS * (s + 1), :] = jnp.broadcast_to(jnp.sum(mine, axis=1, keepdims=True), (PAIRS, 128))
    lay_out(flat, rows, 0, WIDE)
    acc[...] = jnp.zeros(acc.shape, F32)

    def piece(k, carry):
        gate_copy(k).wait()
        up_copy(k).wait()

        @pl.when(k + 3 < PIECES)
        def _():
            gate_copy(k + 3).start()
            up_copy(k + 3).start()

        @pl.when(k + 3 == PIECES)
        def _():
            down_copy.start()

        part = rows[:, cut(k)]
        acc[:, :hidden] += jnp.dot(part, gate[cut(k), :], preferred_element_type=F32)
        acc[:, hidden:] += jnp.dot(part, up[cut(k), :], preferred_element_type=F32)
        return carry

    lax.fori_loop(0, PIECES, piece, 0)
    g, u = acc[:, :hidden], acc[:, hidden:]
    hid[...] = (g / (1.0 + jnp.exp(-g)) * u).astype(BF16)
    down_copy.wait()

    def columns(n, carry):
        value = jnp.dot(hid[...], down[:, cut(n)], preferred_element_type=F32)
        for m in range(PIECE // 128):
            part = value[:, lane_tile(m)] * w_ref[...]
            for s in range(SLOTS):
                at = pl.ds(s * WIDE + PIECE // 128 * n + m, PAIRS, stride=PITCH)
                flat[at, :] = part[PAIRS * s : PAIRS * (s + 1)]
        return carry

    lax.fori_loop(0, PIECES, columns, 0)
    out_ref[...] = flat.reshape(PAIRS, PITCH, 128)[:, :MSG, :].astype(BF16)


def mix_kernel(start, node_in, local_in, msg_in, *refs):
    before, (out_ref, flat_ref, rows_ref, node_ref, local_ref, msg_ref, sum_ref, sem) = refs[:-8], refs[-8:]
    here = [(node_in, node_ref), (local_in, local_ref)] + [(msg_in.at[cut], msg_ref.at[cut]) for cut in CUTS]
    copies = load_all(here + [(old, sum_ref) for old in before], sem)
    copies[0].wait()
    copies[1].wait()
    pick = jnp.concatenate(picks(node_ref, local_ref, start), axis=0).astype(BF16)
    for cut, copy in zip(CUTS, copies[2:]):
        copy.wait()
        flat_ref.reshape(PAIRS, PITCH, 128)[cut, :MSG, :] = msg_ref[cut].astype(F32)
    lay_out(flat_ref, rows_ref, 0, WIDE)
    for copy in copies[6:]:
        copy.wait()
    for k in range(7):
        at = slice(512 * k, 512 * (k + 1))
        value = lax.dot_general(pick, rows_ref[:, at], (((0,), (0,)), ((), ())), preferred_element_type=F32)
        if before:
            value = value + sum_ref[:, at]
        out_ref[:, at] = value.astype(out_ref.dtype)


def in_hbm(array):
    return pltpu.with_memory_space_constraint(array, pltpu.HBM)


def vmem(mib):
    return pltpu.CompilerParams(vmem_limit_bytes=mib << 20)


def step(tokens, node_ids, local_ids, affinity, w_gate, w_up, w_down, grad_parts):
    tok, width = tokens.shape
    hidden = w_gate.shape[2]
    routes = node_ids.T, local_ids.T
    chips, swap = ("edp", "chip"), [(0, 1), (1, 0)]
    core = lax.axis_index("core").astype(I32).reshape(1)
    flat = pltpu.VMEM((PAIRS * PITCH, 128), F32)
    rows = pltpu.VMEM((ROWS, width), BF16)
    far, scalar = pl.BlockSpec(memory_space=pltpu.HBM), pl.BlockSpec(memory_space=pltpu.SMEM)
    local = pl.BlockSpec(memory_space=pltpu.VMEM)
    dma = pltpu.SemaphoreType.DMA
    small = [pltpu.VMEM((4, tok), I32), pltpu.VMEM((8, tok), I32)]

    def exchange(message):
        return lax.all_to_all(message, chips, split_axis=0, concat_axis=0, tiled=True)

    def send(start, *grads):
        shape = (PAIRS, MSG + (GRAD if grads else 0), 128)
        return pl.pallas_call(
            functools.partial(send_kernel, start),
            in_specs=[far] * 4 + [local] * len(grads),
            out_specs=far,
            out_shape=pltpu.HBM(shape, BF16),
            scratch_shapes=[flat, pltpu.VMEM(shape, BF16)]
            + small
            + [pltpu.VMEM((8, tok), F32), pltpu.VMEM((tok, width), BF16), dma((8,))],
            compiler_params=vmem(32),
            name="send",
        )(*map(in_hbm, (*routes, affinity.T, tokens)), *grads)

    def experts(message):
        return pl.pallas_call(
            expert_kernel,
            in_specs=[scalar, local] + [far] * 3,
            out_specs=local,
            out_shape=jax.ShapeDtypeStruct((PAIRS, MSG, 128), BF16),
            scratch_shapes=[
                flat,
                rows,
                pltpu.VMEM((width, hidden), BF16),
                pltpu.VMEM((width, hidden), BF16),
                pltpu.VMEM((hidden, width), BF16),
                pltpu.VMEM((ROWS, 2 * hidden), F32),
                pltpu.VMEM((ROWS, hidden), BF16),
                pltpu.VMEM((ROWS, 128), F32),
                dma((PIECES,)),
                dma((PIECES,)),
                dma((1,)),
            ],
            compiler_params=vmem(40),
            cost_estimate=pl.CostEstimate(
                flops=6 * ROWS * width * hidden, bytes_accessed=6 * width * hidden + 8 * ROWS * width, transcendentals=0
            ),
            name="experts",
        )(core, message, *map(in_hbm, (w_gate, w_up, w_down)))

    def pair_result(message):
        other = lax.ppermute(message, "core", swap)
        mine = experts(message)
        theirs = experts(other)
        back = lax.ppermute(theirs, "core", swap)
        return (mine.astype(F32) + back.astype(F32)).astype(BF16)

    def mix(start, message, *before):
        return pl.pallas_call(
            functools.partial(mix_kernel, start),
            in_specs=[far] * (3 + len(before)),
            out_shape=jax.ShapeDtypeStruct((tok, width), BF16) if before else pltpu.HBM((tok, width), F32),
            scratch_shapes=[flat, rows]
            + small
            + [pltpu.VMEM((PAIRS, MSG, 128), BF16), pltpu.VMEM((tok, width), F32), dma((7,))],
            compiler_params=vmem(32),
            name="mix",
        )(*map(in_hbm, (*routes, message, *before)))

    halves = pl.pallas_call(
        halves_kernel,
        in_specs=[scalar, local],
        out_shape=(
            jax.ShapeDtypeStruct((PAIRS, GRAD, 128), F32),
            jax.ShapeDtypeStruct((PAIRS, GRAD, 128), BF16),
        ),
        compiler_params=vmem(32),
        name="halves",
    )
    keep, give = halves(core, grad_parts[0])
    got = lax.ppermute(give, "core", swap)
    message = send(0)
    arrived = exchange(message)
    message_2 = send(SLOTS, keep, got)
    arrived_2 = exchange(message_2)
    result = pair_result(arrived)
    returned = exchange(result)
    result_2 = pair_result(arrived_2)
    returned_2 = exchange(result_2)
    partial = mix(0, returned)
    mixed = mix(SLOTS, returned_2, partial)
    total = jnp.sum(arrived_2[:, MSG:, :].astype(F32), axis=0)
    low = jnp.concatenate([total[:24], total[24:28]], axis=0)
    high = jnp.concatenate([total[28:], total[:24]], axis=0)
    return mixed, jnp.where(core[0] == 0, low, high)


def solution(mesh):
    split = Mesh(mesh.devices.reshape(2, 32, 2), ("edp", "chip", "core"))
    every = ("edp", "chip", "core")
    flat, deep = P(every, None), P(every, None, None)
    return jax.shard_map(
        step,
        mesh=split,
        in_specs=(flat, flat, flat, flat, deep, deep, deep, deep),
        out_specs=(flat, flat),
        check_vma=False,
    )
```

profile of v0, /device:TPU:10, one launch (start us, length us, event | category | flops | bytes accessed | tf_op | source)
XLA Modules:
  0.0 219.2 jit_solution(15369225738559777652)
XLA Ops:
  0.6 3.9 %send.3 = bf16[64,144,128]{2,1,0:T(8,128)(2,1)} custom-call(s32[4,128]{1,0:T(4,128)} %bitcast.10, s32[8,128]{1,0:T(8,128)} %bitcast.6, f32[8,128]{1,0:T(8,128)} %bitcast.14, bf16[128,3584]{1,0:T(8,128)(2,1)} %tok_in.3), custom_call_target="tpu_custom_call" | custom-call | tf_op jit(solution)/shard_map/send/pallas_call | solution.py:238
  4.5 11.4 %all-to-all-start.2 = ((bf16[64,144,128]{2,1,0:T(8,128)(2,1)}), bf16[64,144,128]{2,1,0:T(8,128)(2,1)S(1)}, u32[]{:S(2)}, u32[]{:S(2)}) async-start(bf16[64,144,128]{2,1,0:T(8,128)(2,1)} %send.3), calls=%async_computation.2 | async-start | bytes 4718592 | tf_op jit(solution)/shard_map/all_to_all | solution.py:234
  15.9 0.0 copy-start.2
  15.9 1.5 copy-done.2
  17.4 0.2 halves.1
  17.6 0.1 collective-permute-start
  17.7 1.9 collective-permute-done.refs_1_
  19.6 4.1 %send.2 = bf16[64,176,128]{2,1,0:T(8,128)(2,1)} custom-call(s32[4,128]{1,0:T(4,128)} %bitcast.11, s32[8,128]{1,0:T(8,128)} %bitcast.7, f32[8,128]{1,0:T(8,128)} %bitcast.15, bf16[128,3584]{1,0:T(8,128)(2,1)} %tok_in.3, f32[64,32,128]{2,1,0:T(8,128)S(1)} %get-tuple-element.4.refs_0_, bf16[64,32,128]{2,1,0:T(8,128)(2,1)S(1)} %collective-permute-done.refs_1_), custom_call_target="tpu_custom_call" | custom-call | tf_op jit(solution)/shard_map/send/pallas_call | solution.py:238
  23.7 22.8 %all-to-all-done.2.in_ref = bf16[64,144,128]{2,1,0:T(8,128)(2,1)S(1)} async-done(((bf16[64,144,128]{2,1,0:T(8,128)(2,1)}), bf16[64,144,128]{2,1,0:T(8,128)(2,1)S(1)}, u32[]{:S(2)}, u32[]{:S(2)}) %all-to-all-start.2) | async-done | bytes 2359328 | tf_op jit(solution)/shard_map/all_to_all | solution.py:234
  46.5 0.0 copy-start
  46.5 1.4 copy-done
  47.9 8.6 %all-to-all-start = ((bf16[64,176,128]{2,1,0:T(8,128)(2,1)}), bf16[64,176,128]{2,1,0:T(8,128)(2,1)S(1)}, u32[]{:S(2)}, u32[]{:S(2)}) async-start(bf16[64,176,128]{2,1,0:T(8,128)(2,1)} %send.2), calls=%async_computation | async-start | bytes 5767168 | tf_op jit(solution)/shard_map/all_to_all | solution.py:234
  56.5 0.1 collective-permute-start.3
  56.6 35.0 %all-to-all-done.in_ref = bf16[64,176,128]{2,1,0:T(8,128)(2,1)S(1)} async-done(((bf16[64,176,128]{2,1,0:T(8,128)(2,1)}), bf16[64,176,128]{2,1,0:T(8,128)(2,1)S(1)}, u32[]{:S(2)}, u32[]{:S(2)}) %all-to-all-start) | async-done | bytes 2883616 | tf_op jit(solution)/shard_map/all_to_all | solution.py:234
  91.5 0.0 collective-permute-start.1
  91.5 0.0 collective-permute-done.3.in_ref
  91.6 14.0 %experts.7 = bf16[64,144,128]{2,1,0:T(8,128)(2,1)S(1)} custom-call(s32[1]{0:T(128)} %bitcast.2.core_ref, bf16[64,144,128]{2,1,0:T(8,128)(2,1)} %collective-permute-done.3.in_ref, bf16[1,3584,1024]{2,1,0:T(8,128)(2,1)} %gate_ref.7, bf16[1,3584,1024]{2,1,0:T(8,128)(2,1)} %up_ref.7, bf16[1,1024,3584]{2,1,0:T(8,128)(2,1)} %down_ref.7), custom_call_target="tpu_custom_call" | custom-call | flops 7046430720 | bytes 31195136 | tf_op jit(solution)/shard_map/experts/pallas_call | solution.py:251
  105.6 0.0 copy-start.1
  105.6 0.8 collective-permute-start.4
  106.4 0.0 collective-permute-done.1.in_ref
  106.4 13.8 %experts.5 = bf16[64,144,128]{2,1,0:T(8,128)(2,1)} custom-call(s32[1]{0:T(128)} %bitcast.2.core_ref, bf16[64,176,128]{2,1,0:T(8,128)(2,1)S(1)} %collective-permute-done.1.in_ref, bf16[1,3584,1024]{2,1,0:T(8,128)(2,1)} %gate_ref.7, bf16[1,3584,1024]{2,1,0:T(8,128)(2,1)} %up_ref.7, bf16[1,1024,3584]{2,1,0:T(8,128)(2,1)} %down_ref.7), custom_call_target="tpu_custom_call" | custom-call | flops 7046430720 | bytes 31195136 | tf_op jit(solution)/shard_map/experts/pallas_call | solution.py:251
  120.2 0.3 collective-permute-start.2
  120.5 0.0 copy-done.1
  120.5 12.7 %experts.6 = bf16[64,144,128]{2,1,0:T(8,128)(2,1)S(1)} custom-call(s32[1]{0:T(128)} %bitcast.2.core_ref, bf16[64,144,128]{2,1,0:T(8,128)(2,1)S(1)} %copy-done.1, bf16[1,3584,1024]{2,1,0:T(8,128)(2,1)} %gate_ref.7, bf16[1,3584,1024]{2,1,0:T(8,128)(2,1)} %up_ref.7, bf16[1,1024,3584]{2,1,0:T(8,128)(2,1)} %down_ref.7), custom_call_target="tpu_custom_call" | custom-call | flops 7046430720 | bytes 31195136 | tf_op jit(solution)/shard_map/experts/pallas_call | solution.py:251
  133.1 0.0 collective-permute-done.4
  133.2 2.2 add_convert_fusion
  135.3 9.4 %all-to-all-start.3 = ((bf16[64,144,128]{2,1,0:T(8,128)(2,1)}), bf16[64,144,128]{2,1,0:T(8,128)(2,1)}, u32[]{:S(2)}, u32[]{:S(2)}) async-start(bf16[64,144,128]{2,1,0:T(8,128)(2,1)} %add_convert_fusion), calls=%async_computation.3 | async-start | bytes 4718592 | tf_op jit(solution)/shard_map/all_to_all | solution.py:234
  144.7 12.7 %experts.4 = bf16[64,144,128]{2,1,0:T(8,128)(2,1)S(1)} custom-call(s32[1]{0:T(128)} %bitcast.2.core_ref, bf16[64,176,128]{2,1,0:T(8,128)(2,1)S(1)} %all-to-all-done.in_ref, bf16[1,3584,1024]{2,1,0:T(8,128)(2,1)} %gate_ref.7, bf16[1,3584,1024]{2,1,0:T(8,128)(2,1)} %up_ref.7, bf16[1,1024,3584]{2,1,0:T(8,128)(2,1)} %down_ref.7), custom_call_target="tpu_custom_call" | custom-call | flops 7046430720 | bytes 31195136 | tf_op jit(solution)/shard_map/experts/pallas_call | solution.py:251
  157.4 0.0 collective-permute-done.2
  157.4 3.7 %add_convert_fusion.1 = bf16[64,144,128]{2,1,0:T(8,128)(2,1)} fusion(bf16[64,144,128]{2,1,0:T(8,128)(2,1)} %collective-permute-done.2, bf16[64,144,128]{2,1,0:T(8,128)(2,1)S(1)} %experts.4), kind=kLoop, calls=%fused_computation.1 | loop fusion | flops 4718592 | bytes 7077888 | tf_op jit(solution)/shard_map/convert_element_type | solution.py:281
  161.1 14.7 %all-to-all-done.3.msg_in = bf16[64,144,128]{2,1,0:T(8,128)(2,1)} async-done(((bf16[64,144,128]{2,1,0:T(8,128)(2,1)}), bf16[64,144,128]{2,1,0:T(8,128)(2,1)}, u32[]{:S(2)}, u32[]{:S(2)}) %all-to-all-start.3) | async-done | bytes 2359328 | tf_op jit(solution)/shard_map/all_to_all | solution.py:234
  175.8 9.4 %all-to-all-start.1 = ((bf16[64,144,128]{2,1,0:T(8,128)(2,1)}), bf16[64,144,128]{2,1,0:T(8,128)(2,1)}, u32[]{:S(2)}, u32[]{:S(2)}) async-start(bf16[64,144,128]{2,1,0:T(8,128)(2,1)} %add_convert_fusion.1), calls=%async_computation.1 | async-start | bytes 4718592 | tf_op jit(solution)/shard_map/all_to_all | solution.py:234
  185.2 0.1 convert_reduce_fusion
  185.4 0.6 slice_select_fusion
  186.0 4.5 %mix.2.refs_0_ = f32[128,3584]{1,0:T(8,128)} custom-call(s32[4,128]{1,0:T(4,128)} %bitcast.12, s32[8,128]{1,0:T(8,128)} %bitcast.8, bf16[64,144,128]{2,1,0:T(8,128)(2,1)} %all-to-all-done.3.msg_in), custom_call_target="tpu_custom_call" | custom-call | tf_op jit(solution)/shard_map/mix/pallas_call | solution.py:284
  190.5 24.3 %all-to-all-done.1.msg_in = bf16[64,144,128]{2,1,0:T(8,128)(2,1)} async-done(((bf16[64,144,128]{2,1,0:T(8,128)(2,1)}), bf16[64,144,128]{2,1,0:T(8,128)(2,1)}, u32[]{:S(2)}, u32[]{:S(2)}) %all-to-all-start.1) | async-done | bytes 2359328 | tf_op jit(solution)/shard_map/all_to_all | solution.py:234
  214.8 4.2 %mix.3 = bf16[128,3584]{1,0:T(8,128)(2,1)} custom-call(s32[4,128]{1,0:T(4,128)} %bitcast.13, s32[8,128]{1,0:T(8,128)} %bitcast.9, bf16[64,144,128]{2,1,0:T(8,128)(2,1)} %all-to-all-done.1.msg_in, f32[128,3584]{1,0:T(8,128)} %mix.2.refs_0_), custom_call_target="tpu_custom_call" | custom-call | tf_op jit(solution)/shard_map/mix/pallas_call | solution.py:284
  (2 shorter events, 0.0 us)
Async XLA Ops:
  4.5 42.0 %all-to-all-start.2 = ((bf16[64,144,128]{2,1,0:T(8,128)(2,1)}), bf16[64,144,128]{2,1,0:T(8,128)(2,1)S(1)}, u32[]{:S(2)}, u32[]{:S(2)}) async-start(bf16[64,144,128]{2,1,0:T(8,128)(2,1)} %send.3), calls=%async_computation.2 | async-start | bytes 4718592 | tf_op jit(solution)/shard_map/all_to_all | solution.py:234
  15.9 1.5 copy-start.2
  17.6 2.0 collective-permute-start
  46.5 1.4 copy-start
  47.9 43.6 %all-to-all-start = ((bf16[64,176,128]{2,1,0:T(8,128)(2,1)}), bf16[64,176,128]{2,1,0:T(8,128)(2,1)S(1)}, u32[]{:S(2)}, u32[]{:S(2)}) async-start(bf16[64,176,128]{2,1,0:T(8,128)(2,1)} %send.2), calls=%async_computation | async-start | bytes 5767168 | tf_op jit(solution)/shard_map/all_to_all | solution.py:234
  56.5 35.1 %collective-permute-start.3 = (bf16[64,144,128]{2,1,0:T(8,128)(2,1)}, bf16[64,144,128]{2,1,0:T(8,128)(2,1)}, u32[]{:S(2)}, u32[]{:S(2)}) collective-permute-start(bf16[64,144,128]{2,1,0:T(8,128)(2,1)} %copy-done), channel_id=1, source_target_pairs={{0,1},{1,0},{2,3},{3,2},{4,5},{5,4},{6,7},{7,6},{8,9},{9,8},{10,11... | collective-permute-start | bytes 7077896 | tf_op jit(solution)/shard_map/ppermute | solution.py:277
  91.5 14.8 %collective-permute-start.1 = (bf16[64,176,128]{2,1,0:T(8,128)(2,1)S(1)}, bf16[64,176,128]{2,1,0:T(8,128)(2,1)S(1)}, u32[]{:S(2)}, u32[]{:S(2)}) collective-permute-start(bf16[64,176,128]{2,1,0:T(8,128)(2,1)S(1)} %all-to-all-done.in_ref), channel_id=1, source_target_pairs={{0,1},{1,0},{2,3},{3,2},{4,5},{5,4},{6,7},{7,6},{8,9},{9,8},{10,11... | collective-permute-start | bytes 8650760 | tf_op jit(solution)/shard_map/ppermute | solution.py:277
  105.6 14.9 %copy-start.1 = (bf16[64,144,128]{2,1,0:T(8,128)(2,1)S(1)}, bf16[64,144,128]{2,1,0:T(8,128)(2,1)}, u32[]{:S(2)}) copy-start(bf16[64,144,128]{2,1,0:T(8,128)(2,1)} %copy-done) | copy-start | bytes 7077892
  105.6 27.6 %collective-permute-start.4 = (bf16[64,144,128]{2,1,0:T(8,128)(2,1)S(1)}, bf16[64,144,128]{2,1,0:T(8,128)(2,1)S(1)}, u32[]{:S(2)}, u32[]{:S(2)}) collective-permute-start(bf16[64,144,128]{2,1,0:T(8,128)(2,1)S(1)} %experts.7), channel_id=1, source_target_pairs={{0,1},{1,0},{2,3},{3,2},{4,5},{5,4},{6,7},{7,6},{8,9},{9,8},{10,11... | collective-permute-start | bytes 7077896 | tf_op jit(solution)/shard_map/ppermute | solution.py:280
  120.2 37.2 %collective-permute-start.2 = (bf16[64,144,128]{2,1,0:T(8,128)(2,1)}, bf16[64,144,128]{2,1,0:T(8,128)(2,1)}, u32[]{:S(2)}, u32[]{:S(2)}) collective-permute-start(bf16[64,144,128]{2,1,0:T(8,128)(2,1)} %experts.5), channel_id=1, source_target_pairs={{0,1},{1,0},{2,3},{3,2},{4,5},{5,4},{6,7},{7,6},{8,9},{9,8},{10,11... | collective-permute-start | bytes 7077896 | tf_op jit(solution)/shard_map/ppermute | solution.py:280
  135.3 40.5 %all-to-all-start.3 = ((bf16[64,144,128]{2,1,0:T(8,128)(2,1)}), bf16[64,144,128]{2,1,0:T(8,128)(2,1)}, u32[]{:S(2)}, u32[]{:S(2)}) async-start(bf16[64,144,128]{2,1,0:T(8,128)(2,1)} %add_convert_fusion), calls=%async_computation.3 | async-start | bytes 4718592 | tf_op jit(solution)/shard_map/all_to_all | solution.py:234
  175.8 38.9 %all-to-all-start.1 = ((bf16[64,144,128]{2,1,0:T(8,128)(2,1)}), bf16[64,144,128]{2,1,0:T(8,128)(2,1)}, u32[]{:S(2)}, u32[]{:S(2)}) async-start(bf16[64,144,128]{2,1,0:T(8,128)(2,1)} %add_convert_fusion.1), calls=%async_computation.1 | async-start | bytes 4718592 | tf_op jit(solution)/shard_map/all_to_all | solution.py:234
where the time goes:
time: 222 us; the launch traced here: 219 us
  waiting for transfers between devices  98.7 us (44%)
  Pallas kernels  70 us (32%)
  starting transfers between devices  39.9 us (18%)
  other arithmetic  6.63 us (3%)
  local copies, waits for them, and re-layouts  2.94 us (1%)
    all_to_all x4, waiting for transfers between devices, exchange(): lax.all_to_all(message, chips, split_axis=0, concat_axis=0, tiled=True)  96.8 us
    pallas_call x4, Pallas kernels, experts(): pl.pallas_call(expert_kernel, in_specs=[scalar, local] + [far] * 3, out_s...  53.2 us
    all_to_all x4, starting transfers between devices, exchange(): lax.all_to_all(message, chips, split_axis=0, concat_axis=0, tiled=True)  38.7 us
    pallas_call x2, Pallas kernels, mix(): pl.pallas_call(functools.partial(mix_kernel, start), in_specs=[far] * (3...  8.76 us
    pallas_call x2, Pallas kernels, send(): pl.pallas_call(functools.partial(send_kernel, start), in_specs=[far] * 4...  7.96 us
    convert_element_type x2, other arithmetic, pair_result(): return (mine.astype(F32) + back.astype(F32)).astype(BF16)  5.91 us
  transfers between devices with their start and end apart: 9, of which 5 were waited for; matrix products, arithmetic and copies ran while one was open for 3% of the time, Pallas kernels for 26%

commit v1 on v0

--- a/solution.py
+++ b/solution.py
@@ -48,8 +48,9 @@
     return copies
 
 
-def send_kernel(start, node_in, local_in, aff_in, tok_in, *refs):
-    grad_refs, (out_ref, flat_ref, stage_ref, node_ref, local_ref, aff_ref, tok_ref, sem) = refs[:-8], refs[-8:]
+def send_kernel(
+    start, node_in, local_in, aff_in, tok_in, out_ref, flat_ref, stage_ref, node_ref, local_ref, aff_ref, tok_ref, sem
+):
     here = ((node_in, node_ref), (local_in, local_ref), (aff_in, aff_ref), (tok_in, tok_ref))
     copies = load_all(here, sem)
     for copy in copies[:3]:
@@ -88,10 +89,7 @@
         flat_ref[pl.ds(row, PAIRS, stride=PITCH), :] = coef
     saves = []
     for i, cut in enumerate(CUTS):
-        stage_ref[cut, :MSG, :] = flat_ref.reshape(PAIRS, PITCH, 128)[cut, :MSG, :].astype(BF16)
-        if grad_refs:
-            keep_ref, got_ref = grad_refs
-            stage_ref[cut, MSG:, :] = (keep_ref[cut] + got_ref[cut].astype(F32)).astype(BF16)
+        stage_ref[cut] = flat_ref.reshape(PAIRS, PITCH, 128)[cut, :MSG, :].astype(BF16)
         saves.append(pltpu.make_async_copy(stage_ref.at[cut], out_ref.at[cut], sem.at[4 + i]))
         saves[-1].start()
     for save in saves:
@@ -120,54 +118,60 @@
             rows_ref[PAIRS * s : PAIRS * (s + 1), lane_tile(j)] = tile.astype(BF16)
 
 
-PIECE, PIECES = 512, 7
+PIECE, PIECES, DEPTH = 512, 7, 4
 
 
 def expert_kernel(
-    core_ref, in_ref, gate_ref, up_ref, down_ref, out_ref,
-    flat, rows, gate, up, down, acc, hid, w_ref, sem_g, sem_u, sem_d,
+    core_ref, own_ref, other_ref, gate_ref, up_ref, down_ref, mine_ref, theirs_ref,
+    flats, rows, gate, up, down, acc, hid, w_ref, sem_g, sem_u, sem_d,
 ):
-    hidden = gate.shape[1]
+    hidden = gate.shape[2]
 
     def cut(k):
         return pl.ds(pl.multiple_of(k * PIECE, PIECE), PIECE)
 
     def gate_copy(k):
-        return pltpu.make_async_copy(gate_ref.at[0, cut(k), :], gate.at[cut(k), :], sem_g.at[k])
+        slot = lax.rem(k, DEPTH)
+        return pltpu.make_async_copy(gate_ref.at[0, cut(k), :], gate.at[slot], sem_g.at[slot])
 
     def up_copy(k):
-        return pltpu.make_async_copy(up_ref.at[0, cut(k), :], up.at[cut(k), :], sem_u.at[k])
+        slot = lax.rem(k, DEPTH)
+        return pltpu.make_async_copy(up_ref.at[0, cut(k), :], up.at[slot], sem_u.at[slot])
 
     down_copy = pltpu.make_async_copy(down_ref.at[0], down, sem_d.at[0])
-    for k in range(3):
+    for k in range(DEPTH - 1):
         gate_copy(k).start()
         up_copy(k).start()
-    spread(in_ref, flat)
     core = core_ref[0]
-    coef = flat[pl.ds(COEF_AT, PAIRS, stride=PITCH), :]
     lane = iota((PAIRS, 128), 1)
-    for s in range(SLOTS):
-        mine = jnp.where(lane // 2 == 2 * s + core, coef, 0.0)
-        w_ref[PAIRS * s : PAIRS * (s + 1), :] = jnp.broadcast_to(jnp.sum(mine, axis=1, keepdims=True), (PAIRS, 128))
-    lay_out(flat, rows, 0, WIDE)
+    for side, in_ref in enumerate((own_ref, other_ref)):
+        flat = flats.at[side]
+        spread(in_ref, flat)
+        coef = flat[pl.ds(COEF_AT, PAIRS, stride=PITCH), :]
+        for s in range(SLOTS):
+            mine = jnp.where(lane // 2 == 2 * s + core, coef, 0.0)
+            at = ROWS * side + PAIRS * s
+            w_ref[at : at + PAIRS, :] = jnp.broadcast_to(jnp.sum(mine, axis=1, keepdims=True), (PAIRS, 128))
+        lay_out(flat, rows.at[ROWS * side : ROWS * (side + 1)], 0, WIDE)
     acc[...] = jnp.zeros(acc.shape, F32)
 
     def piece(k, carry):
+        slot = lax.rem(k, DEPTH)
         gate_copy(k).wait()
         up_copy(k).wait()
 
-        @pl.when(k + 3 < PIECES)
+        @pl.when(k + DEPTH - 1 < PIECES)
         def _():
-            gate_copy(k + 3).start()
-            up_copy(k + 3).start()
-
-        @pl.when(k + 3 == PIECES)
+            gate_copy(k + DEPTH - 1).start()
+            up_copy(k + DEPTH - 1).start()
+
+        @pl.when(k + DEPTH - 1 == PIECES)
         def _():
             down_copy.start()
 
         part = rows[:, cut(k)]
-        acc[:, :hidden] += jnp.dot(part, gate[cut(k), :], preferred_element_type=F32)
-        acc[:, hidden:] += jnp.dot(part, up[cut(k), :], preferred_element_type=F32)
+        acc[:, :hidden] += jnp.dot(part, gate[slot], preferred_element_type=F32)
+        acc[:, hidden:] += jnp.dot(part, up[slot], preferred_element_type=F32)
         return carry
 
     lax.fori_loop(0, PIECES, piece, 0)
@@ -179,27 +183,37 @@
         value = jnp.dot(hid[...], down[:, cut(n)], preferred_element_type=F32)
         for m in range(PIECE // 128):
             part = value[:, lane_tile(m)] * w_ref[...]
-            for s in range(SLOTS):
-                at = pl.ds(s * WIDE + PIECE // 128 * n + m, PAIRS, stride=PITCH)
-                flat[at, :] = part[PAIRS * s : PAIRS * (s + 1)]
+            for s in range(2 * SLOTS):
+                at = pl.ds(s % SLOTS * WIDE + PIECE // 128 * n + m, PAIRS, stride=PITCH)
+                flats[s // SLOTS, at, :] = part[PAIRS * s : PAIRS * (s + 1)]
         return carry
 
     lax.fori_loop(0, PIECES, columns, 0)
-    out_ref[...] = flat.reshape(PAIRS, PITCH, 128)[:, :MSG, :].astype(BF16)
-
-
-def mix_kernel(start, node_in, local_in, msg_in, *refs):
-    before, (out_ref, flat_ref, rows_ref, node_ref, local_ref, msg_ref, sum_ref, sem) = refs[:-8], refs[-8:]
-    here = [(node_in, node_ref), (local_in, local_ref)] + [(msg_in.at[cut], msg_ref.at[cut]) for cut in CUTS]
-    copies = load_all(here + [(old, sum_ref) for old in before], sem)
+    for side, out_ref in enumerate((mine_ref, theirs_ref)):
+        out_ref[...] = flats.at[side].reshape(PAIRS, PITCH, 128)[:, :MSG, :].astype(BF16)
+
+
+def fold_kernel(place_ref, *refs):
+    parts, (total_ref, outs) = refs[:-5], (refs[-1], refs[-5:-1])
+    total = parts[0][...].astype(F32)
+    for part in parts[1:]:
+        total = total + part[...].astype(F32)
+    total_ref[...] = total
+    size = total_ref.shape[0] // 4
+    for flip, out_ref in enumerate(outs):
+        at = jnp.bitwise_xor(place_ref[0], flip) * size
+        out_ref[...] = total_ref[pl.ds(at, size)].astype(out_ref.dtype)
+
+
+def mix_kernel(start, node_in, local_in, in_ref, *refs):
+    before, (out_ref, flat_ref, rows_ref, node_ref, local_ref, sum_ref, sem) = refs[:-7], refs[-7:]
+    copies = load_all([(node_in, node_ref), (local_in, local_ref)] + [(old, sum_ref) for old in before], sem)
     copies[0].wait()
     copies[1].wait()
     pick = jnp.concatenate(picks(node_ref, local_ref, start), axis=0).astype(BF16)
-    for cut, copy in zip(CUTS, copies[2:]):
-        copy.wait()
-        flat_ref.reshape(PAIRS, PITCH, 128)[cut, :MSG, :] = msg_ref[cut].astype(F32)
+    spread(in_ref, flat_ref)
     lay_out(flat_ref, rows_ref, 0, WIDE)
-    for copy in copies[6:]:
+    for copy in copies[2:]:
         copy.wait()
     for k in range(7):
         at = slice(512 * k, 512 * (k + 1))
@@ -213,6 +227,10 @@
     return pltpu.with_memory_space_constraint(array, pltpu.HBM)
 
 
+def place(axes):
+    return lax.axis_index(axes).astype(I32).reshape(1)
+
+
 def vmem(mib):
     return pltpu.CompilerParams(vmem_limit_bytes=mib << 20)
 
@@ -221,8 +239,8 @@
     tok, width = tokens.shape
     hidden = w_gate.shape[2]
     routes = node_ids.T, local_ids.T
-    chips, swap = ("edp", "chip"), [(0, 1), (1, 0)]
-    core = lax.axis_index("core").astype(I32).reshape(1)
+    chips, swap = ("edp", "zh", "x", "y"), [(0, 1), (1, 0)]
+    core = place("core")
     flat = pltpu.VMEM((PAIRS * PITCH, 128), F32)
     rows = pltpu.VMEM((ROWS, width), BF16)
     far, scalar = pl.BlockSpec(memory_space=pltpu.HBM), pl.BlockSpec(memory_space=pltpu.SMEM)
@@ -233,11 +251,11 @@
     def exchange(message):
         return lax.all_to_all(message, chips, split_axis=0, concat_axis=0, tiled=True)
 
-    def send(start, *grads):
-        shape = (PAIRS, MSG + (GRAD if grads else 0), 128)
+    def send(start):
+        shape = (PAIRS, MSG, 128)
         return pl.pallas_call(
             functools.partial(send_kernel, start),
-            in_specs=[far] * 4 + [local] * len(grads),
+            in_specs=[far] * 4,
             out_specs=far,
             out_shape=pltpu.HBM(shape, BF16),
             scratch_shapes=[flat, pltpu.VMEM(shape, BF16)]
@@ -245,52 +263,68 @@
             + [pltpu.VMEM((8, tok), F32), pltpu.VMEM((tok, width), BF16), dma((8,))],
             compiler_params=vmem(32),
             name="send",
-        )(*map(in_hbm, (*routes, affinity.T, tokens)), *grads)
-
-    def experts(message):
+        )(*map(in_hbm, (*routes, affinity.T, tokens)))
+
+    def experts(own, other):
+        shape = jax.ShapeDtypeStruct((PAIRS, MSG, 128), BF16)
         return pl.pallas_call(
             expert_kernel,
-            in_specs=[scalar, local] + [far] * 3,
-            out_specs=local,
-            out_shape=jax.ShapeDtypeStruct((PAIRS, MSG, 128), BF16),
+            in_specs=[scalar, local, local] + [far] * 3,
+            out_specs=(local, local),
+            out_shape=(shape, shape),
             scratch_shapes=[
-                flat,
-                rows,
-                pltpu.VMEM((width, hidden), BF16),
-                pltpu.VMEM((width, hidden), BF16),
+                pltpu.VMEM((2, PAIRS * PITCH, 128), F32),
+                pltpu.VMEM((2 * ROWS, width), BF16),
+                pltpu.VMEM((DEPTH, PIECE, hidden), BF16),
+                pltpu.VMEM((DEPTH, PIECE, hidden), BF16),
                 pltpu.VMEM((hidden, width), BF16),
-                pltpu.VMEM((ROWS, 2 * hidden), F32),
-                pltpu.VMEM((ROWS, hidden), BF16),
-                pltpu.VMEM((ROWS, 128), F32),
-                dma((PIECES,)),
-                dma((PIECES,)),
+                pltpu.VMEM((2 * ROWS, 2 * hidden), F32),
+                pltpu.VMEM((2 * ROWS, hidden), BF16),
+                pltpu.VMEM((2 * ROWS, 128), F32),
+                dma((DEPTH,)),
+                dma((DEPTH,)),
                 dma((1,)),
             ],
-            compiler_params=vmem(40),
+            compiler_params=vmem(46),
             cost_estimate=pl.CostEstimate(
-                flops=6 * ROWS * width * hidden, bytes_accessed=6 * width * hidden + 8 * ROWS * width, transcendentals=0
+                flops=12 * ROWS * width * hidden, bytes_accessed=6 * width * hidden + 16 * ROWS * width, transcendentals=0
             ),
             name="experts",
-        )(core, message, *map(in_hbm, (w_gate, w_up, w_down)))
+        )(core, own, other, *map(in_hbm, (w_gate, w_up, w_down)))
 
     def pair_result(message):
         other = lax.ppermute(message, "core", swap)
-        mine = experts(message)
-        theirs = experts(other)
+        mine, theirs = experts(message, other)
         back = lax.ppermute(theirs, "core", swap)
         return (mine.astype(F32) + back.astype(F32)).astype(BF16)
+
+    def fold(axes, dtype, *parts):
+        size = parts[0].shape[0] // 4
+        shapes = [jax.ShapeDtypeStruct((size, GRAD, 128), F32)] + [jax.ShapeDtypeStruct((size, GRAD, 128), dtype)] * 3
+        kept, *given = pl.pallas_call(
+            fold_kernel,
+            in_specs=[scalar] + [local] * len(parts),
+            out_specs=[local] * 4,
+            out_shape=shapes,
+            scratch_shapes=[pltpu.VMEM(parts[0].shape, F32)],
+            compiler_params=vmem(16),
+            name="fold",
+        )(place(axes), *parts)
+        return [kept] + [
+            lax.ppermute(part, axes, [(i, i ^ flip) for i in range(4)]) for flip, part in enumerate(given, 1)
+        ]
 
     def mix(start, message, *before):
         return pl.pallas_call(
             functools.partial(mix_kernel, start),
-            in_specs=[far] * (3 + len(before)),
+            in_specs=[far, far, local] + [far] * len(before),
             out_shape=jax.ShapeDtypeStruct((tok, width), BF16) if before else pltpu.HBM((tok, width), F32),
             scratch_shapes=[flat, rows]
             + small
-            + [pltpu.VMEM((PAIRS, MSG, 128), BF16), pltpu.VMEM((tok, width), F32), dma((7,))],
+            + [pltpu.VMEM((tok, width), F32), dma((3,))],
             compiler_params=vmem(32),
             name="mix",
-        )(*map(in_hbm, (*routes, message, *before)))
+        )(*map(in_hbm, routes), message, *map(in_hbm, before))
 
     halves = pl.pallas_call(
         halves_kernel,
@@ -304,26 +338,29 @@
     )
     keep, give = halves(core, grad_parts[0])
     got = lax.ppermute(give, "core", swap)
+    parts = fold(("edp", "zh"), BF16, keep, got)
+    parts = fold("x", F32, *parts)
+    parts = fold("y", F32, *parts)
+    total = (parts[0] + parts[1] + parts[2] + parts[3])[0]
+    low = total[:WIDE]
+    high = jnp.concatenate([total[WIDE:], total[:24]], axis=0)
+    router_grad = jnp.where(core[0] == 0, low, high)
     message = send(0)
     arrived = exchange(message)
-    message_2 = send(SLOTS, keep, got)
+    message_2 = send(SLOTS)
     arrived_2 = exchange(message_2)
     result = pair_result(arrived)
     returned = exchange(result)
     result_2 = pair_result(arrived_2)
     returned_2 = exchange(result_2)
     partial = mix(0, returned)
-    mixed = mix(SLOTS, returned_2, partial)
-    total = jnp.sum(arrived_2[:, MSG:, :].astype(F32), axis=0)
-    low = jnp.concatenate([total[:24], total[24:28]], axis=0)
-    high = jnp.concatenate([total[28:], total[:24]], axis=0)
-    return mixed, jnp.where(core[0] == 0, low, high)
+    return mix(SLOTS, returned_2, partial), router_grad
 
 
 def solution(mesh):
-    split = Mesh(mesh.devices.reshape(2, 32, 2), ("edp", "chip", "core"))
-    every = ("edp", "chip", "core")
-    flat, deep = P(every, None), P(every, None, None)
+    axes = ("edp", "zh", "x", "y", "core")
+    split = Mesh(mesh.devices.reshape(2, 2, 4, 4, 2), axes)
+    flat, deep = P(axes, None), P(axes, None, None)
     return jax.shard_map(
         step,
         mesh=split,

time: 222 us -> 256 us (1.15)
  blocking collectives: 0 us -> 82 us
  waiting for transfers between devices: 98.7 us -> 60.4 us
  starting transfers between devices: 39.9 us -> 30.2 us
  Pallas kernels: 70 us -> 67.4 us
    all_to_all x0 -> x2, blocking collectives: none -> 82 us  [exchange(): lax.all_to_all(message, chips, split_axis=0, concat_axis=0, tiled=True)]
    all_to_all x4 -> x2, waiting for transfers between devices: 96.8 us -> 27 us  [exchange(): lax.all_to_all(message, chips, split_axis=0, concat_axis=0, tiled=True)]
    ppermute x0 -> x9, waiting for transfers between devices: none -> 31.1 us  [fold(): lax.ppermute(part, axes, [(i, i ^ flip) for i in range(4)])]
    all_to_all x4 -> x2, starting transfers between devices: 38.7 us -> 17.4 us  [exchange(): lax.all_to_all(message, chips, split_axis=0, concat_axis=0, tiled=True)]
    ppermute x0 -> x9, starting transfers between devices: none -> 12 us  [fold(): lax.ppermute(part, axes, [(i, i ^ flip) for i in range(4)])]
    pallas_call x8 -> x9, Pallas kernels: 69.9 us -> 66.4 us  [the longest x2 47.6 us: experts(): pl.pallas_call(expert_kernel, in_specs=[scalar, local, local] + [far] * 3...]
  transfers between devices with their start and end apart: 9 -> 16, of which waited for: 5 -> 10; matrix products, arithmetic and copies ran while one was open for 3% -> 3% of each run, Pallas kernels for 26% -> 22%
where the time goes in v1:
time: 256 us; the launch traced here: 253 us
  blocking collectives  82 us (32%)
  Pallas kernels  67.4 us (26%)
  waiting for transfers between devices  60.4 us (24%)
  starting transfers between devices  30.2 us (12%)
  other arithmetic  7.24 us (3%)
  local copies, waits for them, and re-layouts  4.58 us (2%)
    all_to_all x2, blocking collectives, exchange(): lax.all_to_all(message, chips, split_axis=0, concat_axis=0, tiled=True)  82 us
    pallas_call x2, Pallas kernels, experts(): pl.pallas_call(expert_kernel, in_specs=[scalar, local, local] + [far] * 3...  47.6 us
    ppermute x9, waiting for transfers between devices, fold(): lax.ppermute(part, axes, [(i, i ^ flip) for i in range(4)])  31.1 us
    all_to_all x2, waiting for transfers between devices, exchange(): lax.all_to_all(message, chips, split_axis=0, concat_axis=0, tiled=True)  27 us
    all_to_all x2, starting transfers between devices, exchange(): lax.all_to_all(message, chips, split_axis=0, concat_axis=0, tiled=True)  17.4 us
    ppermute x9, starting transfers between devices, fold(): lax.ppermute(part, axes, [(i, i ^ flip) for i in range(4)])  12 us
    pallas_call x2, Pallas kernels, mix(): pl.pallas_call(functools.partial(mix_kernel, start), in_specs=[far, far,...  9.09 us
    pallas_call x2, Pallas kernels, send(): pl.pallas_call(functools.partial(send_kernel, start), in_specs=[far] * 4,...  7.72 us
  transfers between devices with their start and end apart: 16, of which 10 were waited for; matrix products, arithmetic and copies ran while one was open for 3% of the time, Pallas kernels for 22%

profile of v1, /device:TPU:10, one launch (start us, length us, event | category | flops | bytes accessed | tf_op | source)
XLA Modules:
  0.0 252.7 jit_solution(5189878655551792257)
XLA Ops:
  0.6 3.9 %send.3 = bf16[64,144,128]{2,1,0:T(8,128)(2,1)} custom-call(s32[4,128]{1,0:T(4,128)} %bitcast.21, s32[8,128]{1,0:T(8,128)} %bitcast.17, f32[8,128]{1,0:T(8,128)} %bitcast.25, bf16[128,3584]{1,0:T(8,128)(2,1)} %tok_in.3), custom_call_target="tpu_custom_call" | custom-call | tf_op jit(solution)/shard_map/send/pallas_call | solution.py:256
  4.5 42.5 %all_to_all.20.own_ref = bf16[64,144,128]{2,1,0:T(8,128)(2,1)S(1)} all-to-all(bf16[64,144,128]{2,1,0:T(8,128)(2,1)} %send.3), channel_id=1, replica_groups=mesh['edp'=2,'zh'=2,'x'=4,'y'=4,'core'=2] {'edp','zh','x','y'}, dimensions={0} | all-to-all | bytes 4718592 | tf_op jit(solution)/shard_map/all_to_all | solution.py:252
  47.0 0.0 collective-permute-start.2
  47.0 3.9 %send.2 = bf16[64,144,128]{2,1,0:T(8,128)(2,1)} custom-call(s32[4,128]{1,0:T(4,128)} %bitcast.22, s32[8,128]{1,0:T(8,128)} %bitcast.18, f32[8,128]{1,0:T(8,128)} %bitcast.26, bf16[128,3584]{1,0:T(8,128)(2,1)} %tok_in.3), custom_call_target="tpu_custom_call" | custom-call | tf_op jit(solution)/shard_map/send/pallas_call | solution.py:256
  50.9 39.5 %all_to_all.21.own_ref = bf16[64,144,128]{2,1,0:T(8,128)(2,1)} all-to-all(bf16[64,144,128]{2,1,0:T(8,128)(2,1)} %send.2), channel_id=1, replica_groups=mesh['edp'=2,'zh'=2,'x'=4,'y'=4,'core'=2] {'edp','zh','x','y'}, dimensions={0} | all-to-all | bytes 4718592 | tf_op jit(solution)/shard_map/all_to_all | solution.py:252
  90.4 0.0 collective-permute-start
  90.4 0.0 collective-permute-done.2.other_ref
  90.4 22.7 %experts.3 = (bf16[64,144,128]{2,1,0:T(8,128)(2,1)S(1)}, bf16[64,144,128]{2,1,0:T(8,128)(2,1)S(1)}) custom-call(s32[1]{0:T(128)} %bitcast.2.core_ref, bf16[64,144,128]{2,1,0:T(8,128)(2,1)S(1)} %all_to_all.20.own_ref, bf16[64,144,128]{2,1,0:T(8,128)(2,1)} %collective-permute-done.2.other_ref, bf16[1,3584,1024]{2,1,0:T(8,128)(2,1)} %gate_ref.3, ...), custom_call_target="tpu_custom_call" | custom-call | flops 14092861440 | bytes 40370176 | tf_op jit(solution)/shard_map/experts/pallas_call | solution.py:270
  113.2 0.8 collective-permute-start.3
  113.9 0.0 collective-permute-done.other_ref
  113.9 24.8 %experts.2 = (bf16[64,144,128]{2,1,0:T(8,128)(2,1)S(1)}, bf16[64,144,128]{2,1,0:T(8,128)(2,1)}) custom-call(s32[1]{0:T(128)} %bitcast.2.core_ref, bf16[64,144,128]{2,1,0:T(8,128)(2,1)} %all_to_all.21.own_ref, bf16[64,144,128]{2,1,0:T(8,128)(2,1)} %collective-permute-done.other_ref, bf16[1,3584,1024]{2,1,0:T(8,128)(2,1)} %gate_ref.3, ...), custom_call_target="tpu_custom_call" | custom-call | flops 14092861440 | bytes 40370176 | tf_op jit(solution)/shard_map/experts/pallas_call | solution.py:270
  138.8 0.0 copy-start
  138.8 1.4 copy-done
  140.2 0.0 collective-permute-start.1
  140.2 0.0 collective-permute-done.3
  140.2 2.2 add_convert_fusion
  142.4 7.9 %all-to-all-start.3 = ((bf16[64,144,128]{2,1,0:T(8,128)(2,1)}), bf16[64,144,128]{2,1,0:T(8,128)(2,1)S(1)}, u32[]{:S(2)}, u32[]{:S(2)}) async-start(bf16[64,144,128]{2,1,0:T(8,128)(2,1)} %add_convert_fusion), calls=%async_computation.3 | async-start | bytes 4718592 | tf_op jit(solution)/shard_map/all_to_all | solution.py:252
  150.4 0.0 collective-permute-done.1
  150.4 4.4 %add_convert_fusion.1 = bf16[64,144,128]{2,1,0:T(8,128)(2,1)} fusion(bf16[64,144,128]{2,1,0:T(8,128)(2,1)} %collective-permute-done.1, bf16[64,144,128]{2,1,0:T(8,128)(2,1)} %copy-done), kind=kLoop, calls=%fused_computation.1 | loop fusion | flops 4718592 | bytes 7077888 | tf_op jit(solution)/shard_map/convert_element_type | solution.py:299
  154.8 27.0 %all-to-all-done.3.in_ref = bf16[64,144,128]{2,1,0:T(8,128)(2,1)S(1)} async-done(((bf16[64,144,128]{2,1,0:T(8,128)(2,1)}), bf16[64,144,128]{2,1,0:T(8,128)(2,1)S(1)}, u32[]{:S(2)}, u32[]{:S(2)}) %all-to-all-start.3) | async-done | bytes 2359328 | tf_op jit(solution)/shard_map/all_to_all | solution.py:252
  181.8 9.4 %all-to-all-start.1 = ((bf16[64,144,128]{2,1,0:T(8,128)(2,1)}), bf16[64,144,128]{2,1,0:T(8,128)(2,1)}, u32[]{:S(2)}, u32[]{:S(2)}) async-start(bf16[64,144,128]{2,1,0:T(8,128)(2,1)} %add_convert_fusion.1), calls=%async_computation.1 | async-start | bytes 4718592 | tf_op jit(solution)/shard_map/all_to_all | solution.py:252
  191.3 0.0 copy-start.1
  191.3 1.5 copy-done.1
  192.8 1.0 halves.1
  193.8 0.0 collective-permute-start.4
  193.8 2.2 collective-permute-done.4.refs_1_
  196.0 1.9 fold.3
  197.9 0.0 copy-start.2
  197.9 0.7 copy-done.2
  198.6 3.0 %collective-permute-start.5 = (bf16[16,32,128]{2,1,0:T(8,128)(2,1)}, bf16[16,32,128]{2,1,0:T(8,128)(2,1)S(1)}, u32[]{:S(2)}, u32[]{:S(2)}) collective-permute-start(bf16[16,32,128]{2,1,0:T(8,128)(2,1)} %get-tuple-element.27), channel_id=1, source_target_pairs={{0,32},{32,0},{64,96},{96,64},{1,33},{33,1},{65,97},{97,65},{2,34}... | collective-permute-start | bytes 393224 | tf_op jit(solution)/shard_map/ppermute | solution.py:314
  201.6 0.8 collective-permute-start.6
  202.4 0.5 collective-permute-start.7
  202.9 20.8 %collective-permute-done.5.refs_1_ = bf16[16,32,128]{2,1,0:T(8,128)(2,1)S(1)} collective-permute-done((bf16[16,32,128]{2,1,0:T(8,128)(2,1)}, bf16[16,32,128]{2,1,0:T(8,128)(2,1)S(1)}, u32[]{:S(2)}, u32[]{:S(2)}) %collective-permute-start.5) | collective-permute-done | bytes 131104 | tf_op jit(solution)/shard_map/ppermute | solution.py:314
  223.7 0.3 collective-permute-done.6.refs_2_
  224.1 0.6 collective-permute-done.7.refs_3_
  224.7 0.0 copy-start.3
  224.7 0.9 copy-done.3
  225.6 0.1 fold.4
  225.7 2.0 collective-permute-start.10
  227.7 1.4 collective-permute-start.8
  229.1 0.2 collective-permute-start.9
  229.3 0.8 collective-permute-done.10.refs_3_
  230.1 2.3 collective-permute-done.8.refs_1_
  232.4 2.4 collective-permute-done.9.refs_2_
  234.9 1.9 collective-permute-start.11
  236.8 2.3 collective-permute-start.12
  239.0 0.0 collective-permute-start.13
  239.0 0.0 collective-permute-done.11
  239.0 3.0 %collective-permute-done.12 = f32[1,32,128]{2,1,0:T(8,128)S(1)} collective-permute-done((f32[1,32,128]{2,1,0:T(8,128)S(1)}, f32[1,32,128]{2,1,0:T(8,128)S(1)}, u32[]{:S(2)}, u32[]{:S(2)}) %collective-permute-start.12) | collective-permute-done | bytes 16416 | tf_op jit(solution)/shard_map/ppermute | solution.py:314
  242.0 0.8 collective-permute-done.13
  242.8 0.6 fusion
  243.4 3.9 %mix.2.refs_0_ = f32[128,3584]{1,0:T(8,128)} custom-call(s32[4,128]{1,0:T(4,128)} %bitcast.23, s32[8,128]{1,0:T(8,128)} %bitcast.19, bf16[64,144,128]{2,1,0:T(8,128)(2,1)S(1)} %all-to-all-done.3.in_ref), custom_call_target="tpu_custom_call" | custom-call | tf_op jit(solution)/shard_map/mix/pallas_call | solution.py:318
  247.3 0.0 all-to-all-done.1.in_ref
  247.3 5.2 %mix.3 = bf16[128,3584]{1,0:T(8,128)(2,1)} custom-call(s32[4,128]{1,0:T(4,128)} %bitcast.24, s32[8,128]{1,0:T(8,128)} %bitcast.20, bf16[64,144,128]{2,1,0:T(8,128)(2,1)} %all-to-all-done.1.in_ref, f32[128,3584]{1,0:T(8,128)} %mix.2.refs_0_), custom_call_target="tpu_custom_call" | custom-call | tf_op jit(solution)/shard_map/mix/pallas_call | solution.py:318
  (4 shorter events, 0.0 us)
Async XLA Ops:
  47.0 43.4 %collective-permute-start.2 = (bf16[64,144,128]{2,1,0:T(8,128)(2,1)S(1)}, bf16[64,144,128]{2,1,0:T(8,128)(2,1)}, u32[]{:S(2)}, u32[]{:S(2)}) collective-permute-start(bf16[64,144,128]{2,1,0:T(8,128)(2,1)S(1)} %all_to_all.20.own_ref), channel_id=1, source_target_pairs={{0,1},{1,0},{2,3},{3,2},{4,5},{5,4},{6,7},{7,6},{8,9},{9,8},{10,11... | collective-permute-start | bytes 7077896 | tf_op jit(solution)/shard_map/ppermute | solution.py:296
  90.4 23.5 %collective-permute-start = (bf16[64,144,128]{2,1,0:T(8,128)(2,1)}, bf16[64,144,128]{2,1,0:T(8,128)(2,1)}, u32[]{:S(2)}, u32[]{:S(2)}) collective-permute-start(bf16[64,144,128]{2,1,0:T(8,128)(2,1)} %all_to_all.21.own_ref), channel_id=1, source_target_pairs={{0,1},{1,0},{2,3},{3,2},{4,5},{5,4},{6,7},{7,6},{8,9},{9,8},{10,11... | collective-permute-start | bytes 7077896 | tf_op jit(solution)/shard_map/ppermute | solution.py:296
  113.2 27.1 %collective-permute-start.3 = (bf16[64,144,128]{2,1,0:T(8,128)(2,1)S(1)}, bf16[64,144,128]{2,1,0:T(8,128)(2,1)S(1)}, u32[]{:S(2)}, u32[]{:S(2)}) collective-permute-start(bf16[64,144,128]{2,1,0:T(8,128)(2,1)S(1)} %get-tuple-element.23), channel_id=1, source_target_pairs={{0,1},{1,0},{2,3},{3,2},{4,5},{5,4},{6,7},{7,6},{8,9},{9,8},{10,11... | collective-permute-start | bytes 7077896 | tf_op jit(solution)/shard_map/ppermute | solution.py:298
  138.8 1.4 copy-start
  140.2 10.2 %collective-permute-start.1 = (bf16[64,144,128]{2,1,0:T(8,128)(2,1)}, bf16[64,144,128]{2,1,0:T(8,128)(2,1)}, u32[]{:S(2)}, u32[]{:S(2)}) collective-permute-start(bf16[64,144,128]{2,1,0:T(8,128)(2,1)} %get-tuple-element.21), channel_id=1, source_target_pairs={{0,1},{1,0},{2,3},{3,2},{4,5},{5,4},{6,7},{7,6},{8,9},{9,8},{10,11... | collective-permute-start | bytes 7077896 | tf_op jit(solution)/shard_map/ppermute | solution.py:298
  142.4 39.4 %all-to-all-start.3 = ((bf16[64,144,128]{2,1,0:T(8,128)(2,1)}), bf16[64,144,128]{2,1,0:T(8,128)(2,1)S(1)}, u32[]{:S(2)}, u32[]{:S(2)}) async-start(bf16[64,144,128]{2,1,0:T(8,128)(2,1)} %add_convert_fusion), calls=%async_computation.3 | async-start | bytes 4718592 | tf_op jit(solution)/shard_map/all_to_all | solution.py:252
  181.8 65.4 %all-to-all-start.1 = ((bf16[64,144,128]{2,1,0:T(8,128)(2,1)}), bf16[64,144,128]{2,1,0:T(8,128)(2,1)}, u32[]{:S(2)}, u32[]{:S(2)}) async-start(bf16[64,144,128]{2,1,0:T(8,128)(2,1)} %add_convert_fusion.1), calls=%async_computation.1 | async-start | bytes 4718592 | tf_op jit(solution)/shard_map/all_to_all | solution.py:252
  191.3 1.5 copy-start.1
  193.8 2.3 collective-permute-start.4
  197.9 0.7 copy-start.2
  198.6 25.1 %collective-permute-start.5 = (bf16[16,32,128]{2,1,0:T(8,128)(2,1)}, bf16[16,32,128]{2,1,0:T(8,128)(2,1)S(1)}, u32[]{:S(2)}, u32[]{:S(2)}) collective-permute-start(bf16[16,32,128]{2,1,0:T(8,128)(2,1)} %get-tuple-element.27), channel_id=1, source_target_pairs={{0,32},{32,0},{64,96},{96,64},{1,33},{33,1},{65,97},{97,65},{2,34}... | collective-permute-start | bytes 393224 | tf_op jit(solution)/shard_map/ppermute | solution.py:314
  201.6 22.4 %collective-permute-start.6 = (bf16[16,32,128]{2,1,0:T(8,128)(2,1)}, bf16[16,32,128]{2,1,0:T(8,128)(2,1)S(1)}, u32[]{:S(2)}, u32[]{:S(2)}) collective-permute-start(bf16[16,32,128]{2,1,0:T(8,128)(2,1)} %get-tuple-element.28), channel_id=1, source_target_pairs={{0,64},{32,96},{64,0},{96,32},{1,65},{33,97},{65,1},{97,33},{2,66}... | collective-permute-start | bytes 393224 | tf_op jit(solution)/shard_map/ppermute | solution.py:314
  202.4 22.3 %collective-permute-start.7 = (bf16[16,32,128]{2,1,0:T(8,128)(2,1)S(1)}, bf16[16,32,128]{2,1,0:T(8,128)(2,1)S(1)}, u32[]{:S(2)}, u32[]{:S(2)}) collective-permute-start(bf16[16,32,128]{2,1,0:T(8,128)(2,1)S(1)} %get-tuple-element.29), channel_id=1, source_target_pairs={{0,96},{32,64},{64,32},{96,0},{1,97},{33,65},{65,33},{97,1},{2,98}... | collective-permute-start | bytes 393224 | tf_op jit(solution)/shard_map/ppermute | solution.py:314
  224.7 1.0 copy-start.3
  225.7 4.4 %collective-permute-start.10 = (f32[4,32,128]{2,1,0:T(8,128)S(1)}, f32[4,32,128]{2,1,0:T(8,128)S(1)}, u32[]{:S(2)}, u32[]{:S(2)}) collective-permute-start(f32[4,32,128]{2,1,0:T(8,128)S(1)} %get-tuple-element.33), channel_id=1, source_target_pairs={{0,24},{8,16},{16,8},{24,0},{1,25},{9,17},{17,9},{25,1},{2,26},{10... | collective-permute-start | bytes 196616 | tf_op jit(solution)/shard_map/ppermute | solution.py:314
  227.7 4.7 %collective-permute-start.8 = (f32[4,32,128]{2,1,0:T(8,128)S(1)}, f32[4,32,128]{2,1,0:T(8,128)S(1)}, u32[]{:S(2)}, u32[]{:S(2)}) collective-permute-start(f32[4,32,128]{2,1,0:T(8,128)S(1)} %get-tuple-element.31), channel_id=1, source_target_pairs={{0,8},{8,0},{16,24},{24,16},{1,9},{9,1},{17,25},{25,17},{2,10},{10... | collective-permute-start | bytes 196616 | tf_op jit(solution)/shard_map/ppermute | solution.py:314
  229.1 5.8 %collective-permute-start.9 = (f32[4,32,128]{2,1,0:T(8,128)S(1)}, f32[4,32,128]{2,1,0:T(8,128)S(1)}, u32[]{:S(2)}, u32[]{:S(2)}) collective-permute-start(f32[4,32,128]{2,1,0:T(8,128)S(1)} %get-tuple-element.32), channel_id=1, source_target_pairs={{0,16},{8,24},{16,0},{24,8},{1,17},{9,25},{17,1},{25,9},{2,18},{10... | collective-permute-start | bytes 196616 | tf_op jit(solution)/shard_map/ppermute | solution.py:314
  234.9 4.2 %collective-permute-start.11 = (f32[1,32,128]{2,1,0:T(8,128)S(1)}, f32[1,32,128]{2,1,0:T(8,128)S(1)}, u32[]{:S(2)}, u32[]{:S(2)}) collective-permute-start(f32[1,32,128]{2,1,0:T(8,128)S(1)} %get-tuple-element.35), channel_id=1, source_target_pairs={{0,2},{2,0},{4,6},{6,4},{1,3},{3,1},{5,7},{7,5},{8,10},{10,8},{12,... | collective-permute-start | bytes 49160 | tf_op jit(solution)/shard_map/ppermute | solution.py:314
  236.8 5.2 %collective-permute-start.12 = (f32[1,32,128]{2,1,0:T(8,128)S(1)}, f32[1,32,128]{2,1,0:T(8,128)S(1)}, u32[]{:S(2)}, u32[]{:S(2)}) collective-permute-start(f32[1,32,128]{2,1,0:T(8,128)S(1)} %get-tuple-element.36), channel_id=1, source_target_pairs={{0,4},{2,6},{4,0},{6,2},{1,5},{3,7},{5,1},{7,3},{8,12},{10,14},{12... | collective-permute-start | bytes 49160 | tf_op jit(solution)/shard_map/ppermute | solution.py:314
  239.0 3.7 %collective-permute-start.13 = (f32[1,32,128]{2,1,0:T(8,128)S(1)}, f32[1,32,128]{2,1,0:T(8,128)S(1)}, u32[]{:S(2)}, u32[]{:S(2)}) collective-permute-start(f32[1,32,128]{2,1,0:T(8,128)S(1)} %get-tuple-element.37), channel_id=1, source_target_pairs={{0,6},{2,4},{4,2},{6,0},{1,7},{3,5},{5,3},{7,1},{8,14},{10,12},{12... | collective-permute-start | bytes 49160 | tf_op jit(solution)/shard_map/ppermute | solution.py:314

commit v2 on v1

--- a/solution.py
+++ b/solution.py
@@ -118,79 +118,101 @@
             rows_ref[PAIRS * s : PAIRS * (s + 1), lane_tile(j)] = tile.astype(BF16)
 
 
-PIECE, PIECES, DEPTH = 512, 7, 4
+PIECE, PIECES, BLOCK = 1792, 2, 512
 
 
 def expert_kernel(
     core_ref, own_ref, other_ref, gate_ref, up_ref, down_ref, mine_ref, theirs_ref,
-    flats, rows, gate, up, down, acc, hid, w_ref, sem_g, sem_u, sem_d,
+    flat, rows, gate, up, down, acc, hid, w_ref, sem_g, sem_u, sem_d,
 ):
     hidden = gate.shape[2]
 
-    def cut(k):
-        return pl.ds(pl.multiple_of(k * PIECE, PIECE), PIECE)
-
-    def gate_copy(k):
-        slot = lax.rem(k, DEPTH)
-        return pltpu.make_async_copy(gate_ref.at[0, cut(k), :], gate.at[slot], sem_g.at[slot])
-
-    def up_copy(k):
-        slot = lax.rem(k, DEPTH)
-        return pltpu.make_async_copy(up_ref.at[0, cut(k), :], up.at[slot], sem_u.at[slot])
-
+    def copies(k):
+        at = pl.ds(pl.multiple_of(k * PIECE, PIECE), PIECE)
+        return (
+            pltpu.make_async_copy(gate_ref.at[0, at, :], gate.at[k], sem_g.at[k]),
+            pltpu.make_async_copy(up_ref.at[0, at, :], up.at[k], sem_u.at[k]),
+        )
+
+    for k in range(PIECES):
+        for copy in copies(k):
+            copy.start()
     down_copy = pltpu.make_async_copy(down_ref.at[0], down, sem_d.at[0])
-    for k in range(DEPTH - 1):
-        gate_copy(k).start()
-        up_copy(k).start()
+    down_copy.start()
     core = core_ref[0]
     lane = iota((PAIRS, 128), 1)
     for side, in_ref in enumerate((own_ref, other_ref)):
-        flat = flats.at[side]
         spread(in_ref, flat)
         coef = flat[pl.ds(COEF_AT, PAIRS, stride=PITCH), :]
         for s in range(SLOTS):
             mine = jnp.where(lane // 2 == 2 * s + core, coef, 0.0)
             at = ROWS * side + PAIRS * s
             w_ref[at : at + PAIRS, :] = jnp.broadcast_to(jnp.sum(mine, axis=1, keepdims=True), (PAIRS, 128))
-        lay_out(flat, rows.at[ROWS * side : ROWS * (side + 1)], 0, WIDE)
+        for s in range(SLOTS):
+            at = ROWS * side + PAIRS * s
+            for j in range(WIDE):
+                tile = flat[pl.ds(s * WIDE + j, PAIRS, stride=PITCH), :]
+                half = WIDE // PIECES
+                rows[j // half, at : at + PAIRS, lane_tile(j % half)] = tile.astype(BF16)
     acc[...] = jnp.zeros(acc.shape, F32)
 
     def piece(k, carry):
-        slot = lax.rem(k, DEPTH)
-        gate_copy(k).wait()
-        up_copy(k).wait()
-
-        @pl.when(k + DEPTH - 1 < PIECES)
-        def _():
-            gate_copy(k + DEPTH - 1).start()
-            up_copy(k + DEPTH - 1).start()
-
-        @pl.when(k + DEPTH - 1 == PIECES)
-        def _():
-            down_copy.start()
-
-        part = rows[:, cut(k)]
-        acc[:, :hidden] += jnp.dot(part, gate[slot], preferred_element_type=F32)
-        acc[:, hidden:] += jnp.dot(part, up[slot], preferred_element_type=F32)
+        for copy in copies(k):
+            copy.wait()
+        acc[:, :hidden] += jnp.dot(rows[k], gate[k], preferred_element_type=F32)
+        acc[:, hidden:] += jnp.dot(rows[k], up[k], preferred_element_type=F32)
         return carry
 
     lax.fori_loop(0, PIECES, piece, 0)
-    g, u = acc[:, :hidden], acc[:, hidden:]
-    hid[...] = (g / (1.0 + jnp.exp(-g)) * u).astype(BF16)
+    for n in range(0, hidden, 256):
+        g, u = acc[:, n : n + 256], acc[:, hidden + n : hidden + n + 256]
+        hid[:, n : n + 256] = (g / (1.0 + jnp.exp(-g)) * u).astype(BF16)
     down_copy.wait()
-
-    def columns(n, carry):
-        value = jnp.dot(hid[...], down[:, cut(n)], preferred_element_type=F32)
-        for m in range(PIECE // 128):
-            part = value[:, lane_tile(m)] * w_ref[...]
-            for s in range(2 * SLOTS):
-                at = pl.ds(s % SLOTS * WIDE + PIECE // 128 * n + m, PAIRS, stride=PITCH)
-                flats[s // SLOTS, at, :] = part[PAIRS * s : PAIRS * (s + 1)]
-        return carry
-
-    lax.fori_loop(0, PIECES, columns, 0)
     for side, out_ref in enumerate((mine_ref, theirs_ref)):
-        out_ref[...] = flats.at[side].reshape(PAIRS, PITCH, 128)[:, :MSG, :].astype(BF16)
+        here = slice(ROWS * side, ROWS * (side + 1))
+
+        def columns(n, carry):
+            at = pl.ds(pl.multiple_of(n * BLOCK, BLOCK), BLOCK)
+            value = jnp.dot(hid[here, :], down[:, at], preferred_element_type=F32)
+            for m in range(BLOCK // 128):
+                part = value[:, lane_tile(m)] * w_ref[here, :]
+                for s in range(SLOTS):
+                    to = pl.ds(s * WIDE + BLOCK // 128 * n + m, PAIRS, stride=PITCH)
+                    flat[to, :] = part[PAIRS * s : PAIRS * (s + 1)]
+            return carry
+
+        lax.fori_loop(0, down.shape[1] // BLOCK, columns, 0)
+        out_ref[...] = flat.reshape(PAIRS, PITCH, 128)[:, :MSG, :].astype(BF16)
+
+
+def expert_call(width, hidden):
+    scalar, local = pl.BlockSpec(memory_space=pltpu.SMEM), pl.BlockSpec(memory_space=pltpu.VMEM)
+    far, dma = pl.BlockSpec(memory_space=pltpu.HBM), pltpu.SemaphoreType.DMA
+    shape = jax.ShapeDtypeStruct((PAIRS, MSG, 128), BF16)
+    return pl.pallas_call(
+        expert_kernel,
+        in_specs=[scalar, local, local] + [far] * 3,
+        out_specs=(local, local),
+        out_shape=(shape, shape),
+        scratch_shapes=[
+            pltpu.VMEM((PAIRS * PITCH, 128), F32),
+            pltpu.VMEM((PIECES, 2 * ROWS, PIECE), BF16),
+            pltpu.VMEM((PIECES, PIECE, hidden), BF16),
+            pltpu.VMEM((PIECES, PIECE, hidden), BF16),
+            pltpu.VMEM((hidden, width), BF16),
+            pltpu.VMEM((2 * ROWS, 2 * hidden), F32),
+            pltpu.VMEM((2 * ROWS, hidden), BF16),
+            pltpu.VMEM((2 * ROWS, 128), F32),
+            dma((PIECES,)),
+            dma((PIECES,)),
+            dma((1,)),
+        ],
+        compiler_params=vmem(44),
+        cost_estimate=pl.CostEstimate(
+            flops=12 * ROWS * width * hidden, bytes_accessed=6 * width * hidden + 16 * ROWS * width, transcendentals=0
+        ),
+        name="experts",
+    )
 
 
 def fold_kernel(place_ref, *refs):
@@ -266,31 +288,7 @@
         )(*map(in_hbm, (*routes, affinity.T, tokens)))
 
     def experts(own, other):
-        shape = jax.ShapeDtypeStruct((PAIRS, MSG, 128), BF16)
-        return pl.pallas_call(
-            expert_kernel,
-            in_specs=[scalar, local, local] + [far] * 3,
-            out_specs=(local, local),
-            out_shape=(shape, shape),
-            scratch_shapes=[
-                pltpu.VMEM((2, PAIRS * PITCH, 128), F32),
-                pltpu.VMEM((2 * ROWS, width), BF16),
-                pltpu.VMEM((DEPTH, PIECE, hidden), BF16),
-                pltpu.VMEM((DEPTH, PIECE, hidden), BF16),
-                pltpu.VMEM((hidden, width), BF16),
-                pltpu.VMEM((2 * ROWS, 2 * hidden), F32),
-                pltpu.VMEM((2 * ROWS, hidden), BF16),
-                pltpu.VMEM((2 * ROWS, 128), F32),
-                dma((DEPTH,)),
-                dma((DEPTH,)),
-                dma((1,)),
-            ],
-            compiler_params=vmem(46),
-            cost_estimate=pl.CostEstimate(
-                flops=12 * ROWS * width * hidden, bytes_accessed=6 * width * hidden + 16 * ROWS * width, transcendentals=0
-            ),
-            name="experts",
-        )(core, own, other, *map(in_hbm, (w_gate, w_up, w_down)))
+        return expert_call(width, hidden)(core, own, other, *map(in_hbm, (w_gate, w_up, w_down)))
 
     def pair_result(message):
         other = lax.ppermute(message, "core", swap)

time: 256 us -> 257 us (level)
  no operation moved by 1% of the time
where the time goes in v2:
time: 257 us; the launch traced here: 254 us
  blocking collectives  82 us (32%)
  Pallas kernels  68.7 us (27%)
  waiting for transfers between devices  60.4 us (24%)
  starting transfers between devices  30 us (12%)
  other arithmetic  7.24 us (3%)
  local copies, waits for them, and re-layouts  4.58 us (2%)
    all_to_all x2, blocking collectives, exchange(): lax.all_to_all(message, chips, split_axis=0, concat_axis=0, tiled=True)  82 us
    pallas_call x2, Pallas kernels, experts(): expert_call(width, hidden)  48.9 us
    ppermute x9, waiting for transfers between devices, fold(): lax.ppermute(part, axes, [(i, i ^ flip) for i in range(4)])  31.1 us
    all_to_all x2, waiting for transfers between devices, exchange(): lax.all_to_all(message, chips, split_axis=0, concat_axis=0, tiled=True)  27 us
    all_to_all x2, starting transfers between devices, exchange(): lax.all_to_all(message, chips, split_axis=0, concat_axis=0, tiled=True)  17.4 us
    ppermute x9, starting transfers between devices, fold(): lax.ppermute(part, axes, [(i, i ^ flip) for i in range(4)])  11.8 us
    pallas_call x2, Pallas kernels, mix(): pl.pallas_call(functools.partial(mix_kernel, start), in_specs=[far, far,...  9.1 us
    pallas_call x2, Pallas kernels, send(): pl.pallas_call(functools.partial(send_kernel, start), in_specs=[far] * 4,...  7.72 us
  transfers between devices with their start and end apart: 16, of which 10 were waited for; matrix products, arithmetic and copies ran while one was open for 3% of the time, Pallas kernels for 22%

profile of v2, /device:TPU:10, one launch (start us, length us, event | category | flops | bytes accessed | tf_op | source)
XLA Modules:
  0.0 253.8 jit_solution(3823222501713538759)
XLA Ops:
  0.6 3.9 %send.3 = bf16[64,144,128]{2,1,0:T(8,128)(2,1)} custom-call(s32[4,128]{1,0:T(4,128)} %bitcast.21, s32[8,128]{1,0:T(8,128)} %bitcast.17, f32[8,128]{1,0:T(8,128)} %bitcast.25, bf16[128,3584]{1,0:T(8,128)(2,1)} %tok_in.3), custom_call_target="tpu_custom_call" | custom-call | tf_op jit(solution)/shard_map/send/pallas_call | solution.py:278
  4.5 42.5 %all_to_all.20.own_ref = bf16[64,144,128]{2,1,0:T(8,128)(2,1)S(1)} all-to-all(bf16[64,144,128]{2,1,0:T(8,128)(2,1)} %send.3), channel_id=1, replica_groups=mesh['edp'=2,'zh'=2,'x'=4,'y'=4,'core'=2] {'edp','zh','x','y'}, dimensions={0} | all-to-all | bytes 4718592 | tf_op jit(solution)/shard_map/all_to_all | solution.py:274
  47.0 0.0 collective-permute-start.2
  47.0 3.9 %send.2 = bf16[64,144,128]{2,1,0:T(8,128)(2,1)} custom-call(s32[4,128]{1,0:T(4,128)} %bitcast.22, s32[8,128]{1,0:T(8,128)} %bitcast.18, f32[8,128]{1,0:T(8,128)} %bitcast.26, bf16[128,3584]{1,0:T(8,128)(2,1)} %tok_in.3), custom_call_target="tpu_custom_call" | custom-call | tf_op jit(solution)/shard_map/send/pallas_call | solution.py:278
  50.9 39.5 %all_to_all.21.own_ref = bf16[64,144,128]{2,1,0:T(8,128)(2,1)} all-to-all(bf16[64,144,128]{2,1,0:T(8,128)(2,1)} %send.2), channel_id=1, replica_groups=mesh['edp'=2,'zh'=2,'x'=4,'y'=4,'core'=2] {'edp','zh','x','y'}, dimensions={0} | all-to-all | bytes 4718592 | tf_op jit(solution)/shard_map/all_to_all | solution.py:274
  90.4 0.0 collective-permute-start
  90.4 0.0 collective-permute-done.2.other_ref
  90.4 23.4 %experts.3 = (bf16[64,144,128]{2,1,0:T(8,128)(2,1)S(1)}, bf16[64,144,128]{2,1,0:T(8,128)(2,1)S(1)}) custom-call(s32[1]{0:T(128)} %bitcast.2.core_ref, bf16[64,144,128]{2,1,0:T(8,128)(2,1)S(1)} %all_to_all.20.own_ref, bf16[64,144,128]{2,1,0:T(8,128)(2,1)} %collective-permute-done.2.other_ref, bf16[1,3584,1024]{2,1,0:T(8,128)(2,1)} %gate_ref.3, ...), custom_call_target="tpu_custom_call" | custom-call | flops 14092861440 | bytes 40370176 | tf_op jit(solution)/shard_map/experts/pallas_call | solution.py:291
  113.8 0.8 collective-permute-start.3
  114.6 0.0 collective-permute-done.other_ref
  114.6 25.5 %experts.2 = (bf16[64,144,128]{2,1,0:T(8,128)(2,1)S(1)}, bf16[64,144,128]{2,1,0:T(8,128)(2,1)}) custom-call(s32[1]{0:T(128)} %bitcast.2.core_ref, bf16[64,144,128]{2,1,0:T(8,128)(2,1)} %all_to_all.21.own_ref, bf16[64,144,128]{2,1,0:T(8,128)(2,1)} %collective-permute-done.other_ref, bf16[1,3584,1024]{2,1,0:T(8,128)(2,1)} %gate_ref.3, ...), custom_call_target="tpu_custom_call" | custom-call | flops 14092861440 | bytes 40370176 | tf_op jit(solution)/shard_map/experts/pallas_call | solution.py:291
  140.1 0.0 copy-start
  140.1 1.4 copy-done
  141.5 0.0 collective-permute-start.1
  141.6 0.0 collective-permute-done.3
  141.6 2.2 add_convert_fusion
  143.8 7.9 %all-to-all-start.3 = ((bf16[64,144,128]{2,1,0:T(8,128)(2,1)}), bf16[64,144,128]{2,1,0:T(8,128)(2,1)S(1)}, u32[]{:S(2)}, u32[]{:S(2)}) async-start(bf16[64,144,128]{2,1,0:T(8,128)(2,1)} %add_convert_fusion), calls=%async_computation.3 | async-start | bytes 4718592 | tf_op jit(solution)/shard_map/all_to_all | solution.py:274
  151.7 0.0 collective-permute-done.1
  151.7 4.4 %add_convert_fusion.1 = bf16[64,144,128]{2,1,0:T(8,128)(2,1)} fusion(bf16[64,144,128]{2,1,0:T(8,128)(2,1)} %collective-permute-done.1, bf16[64,144,128]{2,1,0:T(8,128)(2,1)} %copy-done), kind=kLoop, calls=%fused_computation.1 | loop fusion | flops 4718592 | bytes 7077888 | tf_op jit(solution)/shard_map/convert_element_type | solution.py:297
  156.1 27.0 %all-to-all-done.3.in_ref = bf16[64,144,128]{2,1,0:T(8,128)(2,1)S(1)} async-done(((bf16[64,144,128]{2,1,0:T(8,128)(2,1)}), bf16[64,144,128]{2,1,0:T(8,128)(2,1)S(1)}, u32[]{:S(2)}, u32[]{:S(2)}) %all-to-all-start.3) | async-done | bytes 2359328 | tf_op jit(solution)/shard_map/all_to_all | solution.py:274
  183.2 9.4 %all-to-all-start.1 = ((bf16[64,144,128]{2,1,0:T(8,128)(2,1)}), bf16[64,144,128]{2,1,0:T(8,128)(2,1)}, u32[]{:S(2)}, u32[]{:S(2)}) async-start(bf16[64,144,128]{2,1,0:T(8,128)(2,1)} %add_convert_fusion.1), calls=%async_computation.1 | async-start | bytes 4718592 | tf_op jit(solution)/shard_map/all_to_all | solution.py:274
  192.6 0.0 copy-start.1
  192.6 1.5 copy-done.1
  194.1 1.0 halves.1
  195.1 0.0 collective-permute-start.4
  195.1 2.2 collective-permute-done.4.refs_1_
  197.3 1.9 fold.3
  199.3 0.0 copy-start.2
  199.3 0.7 copy-done.2
  200.0 3.0 %collective-permute-start.5 = (bf16[16,32,128]{2,1,0:T(8,128)(2,1)}, bf16[16,32,128]{2,1,0:T(8,128)(2,1)S(1)}, u32[]{:S(2)}, u32[]{:S(2)}) collective-permute-start(bf16[16,32,128]{2,1,0:T(8,128)(2,1)} %get-tuple-element.27), channel_id=1, source_target_pairs={{0,32},{32,0},{64,96},{96,64},{1,33},{33,1},{65,97},{97,65},{2,34}... | collective-permute-start | bytes 393224 | tf_op jit(solution)/shard_map/ppermute | solution.py:312
  203.0 0.8 collective-permute-start.6
  203.7 0.5 collective-permute-start.7
  204.2 20.8 %collective-permute-done.5.refs_1_ = bf16[16,32,128]{2,1,0:T(8,128)(2,1)S(1)} collective-permute-done((bf16[16,32,128]{2,1,0:T(8,128)(2,1)}, bf16[16,32,128]{2,1,0:T(8,128)(2,1)S(1)}, u32[]{:S(2)}, u32[]{:S(2)}) %collective-permute-start.5) | collective-permute-done | bytes 131104 | tf_op jit(solution)/shard_map/ppermute | solution.py:312
  225.1 0.3 collective-permute-done.6.refs_2_
  225.4 0.6 collective-permute-done.7.refs_3_
  226.0 0.0 copy-start.3
  226.0 0.9 copy-done.3
  226.9 0.1 fold.4
  227.0 2.0 collective-permute-start.10
  229.0 1.4 collective-permute-start.8
  230.4 0.2 collective-permute-start.9
  230.6 0.8 collective-permute-done.10.refs_3_
  231.4 2.3 collective-permute-done.8.refs_1_
  233.7 2.4 collective-permute-done.9.refs_2_
  236.2 1.7 collective-permute-start.11
  237.9 2.3 collective-permute-start.12
  240.1 0.0 collective-permute-start.13
  240.2 0.0 collective-permute-done.11
  240.2 3.0 %collective-permute-done.12 = f32[1,32,128]{2,1,0:T(8,128)S(1)} collective-permute-done((f32[1,32,128]{2,1,0:T(8,128)S(1)}, f32[1,32,128]{2,1,0:T(8,128)S(1)}, u32[]{:S(2)}, u32[]{:S(2)}) %collective-permute-start.12) | collective-permute-done | bytes 16416 | tf_op jit(solution)/shard_map/ppermute | solution.py:312
  243.1 0.8 collective-permute-done.13
  243.9 0.6 fusion
  244.5 3.9 %mix.2.refs_0_ = f32[128,3584]{1,0:T(8,128)} custom-call(s32[4,128]{1,0:T(4,128)} %bitcast.23, s32[8,128]{1,0:T(8,128)} %bitcast.19, bf16[64,144,128]{2,1,0:T(8,128)(2,1)S(1)} %all-to-all-done.3.in_ref), custom_call_target="tpu_custom_call" | custom-call | tf_op jit(solution)/shard_map/mix/pallas_call | solution.py:316
  248.4 0.0 all-to-all-done.1.in_ref
  248.4 5.2 %mix.3 = bf16[128,3584]{1,0:T(8,128)(2,1)} custom-call(s32[4,128]{1,0:T(4,128)} %bitcast.24, s32[8,128]{1,0:T(8,128)} %bitcast.20, bf16[64,144,128]{2,1,0:T(8,128)(2,1)} %all-to-all-done.1.in_ref, f32[128,3584]{1,0:T(8,128)} %mix.2.refs_0_), custom_call_target="tpu_custom_call" | custom-call | tf_op jit(solution)/shard_map/mix/pallas_call | solution.py:316
  (4 shorter events, 0.0 us)
Async XLA Ops:
  47.0 43.4 %collective-permute-start.2 = (bf16[64,144,128]{2,1,0:T(8,128)(2,1)S(1)}, bf16[64,144,128]{2,1,0:T(8,128)(2,1)}, u32[]{:S(2)}, u32[]{:S(2)}) collective-permute-start(bf16[64,144,128]{2,1,0:T(8,128)(2,1)S(1)} %all_to_all.20.own_ref), channel_id=1, source_target_pairs={{0,1},{1,0},{2,3},{3,2},{4,5},{5,4},{6,7},{7,6},{8,9},{9,8},{10,11... | collective-permute-start | bytes 7077896 | tf_op jit(solution)/shard_map/ppermute | solution.py:294
  90.4 24.2 %collective-permute-start = (bf16[64,144,128]{2,1,0:T(8,128)(2,1)}, bf16[64,144,128]{2,1,0:T(8,128)(2,1)}, u32[]{:S(2)}, u32[]{:S(2)}) collective-permute-start(bf16[64,144,128]{2,1,0:T(8,128)(2,1)} %all_to_all.21.own_ref), channel_id=1, source_target_pairs={{0,1},{1,0},{2,3},{3,2},{4,5},{5,4},{6,7},{7,6},{8,9},{9,8},{10,11... | collective-permute-start | bytes 7077896 | tf_op jit(solution)/shard_map/ppermute | solution.py:294
  113.8 27.8 %collective-permute-start.3 = (bf16[64,144,128]{2,1,0:T(8,128)(2,1)S(1)}, bf16[64,144,128]{2,1,0:T(8,128)(2,1)S(1)}, u32[]{:S(2)}, u32[]{:S(2)}) collective-permute-start(bf16[64,144,128]{2,1,0:T(8,128)(2,1)S(1)} %get-tuple-element.23), channel_id=1, source_target_pairs={{0,1},{1,0},{2,3},{3,2},{4,5},{5,4},{6,7},{7,6},{8,9},{9,8},{10,11... | collective-permute-start | bytes 7077896 | tf_op jit(solution)/shard_map/ppermute | solution.py:296
  140.1 1.4 copy-start
  141.5 10.2 %collective-permute-start.1 = (bf16[64,144,128]{2,1,0:T(8,128)(2,1)}, bf16[64,144,128]{2,1,0:T(8,128)(2,1)}, u32[]{:S(2)}, u32[]{:S(2)}) collective-permute-start(bf16[64,144,128]{2,1,0:T(8,128)(2,1)} %get-tuple-element.21), channel_id=1, source_target_pairs={{0,1},{1,0},{2,3},{3,2},{4,5},{5,4},{6,7},{7,6},{8,9},{9,8},{10,11... | collective-permute-start | bytes 7077896 | tf_op jit(solution)/shard_map/ppermute | solution.py:296
  143.8 39.4 %all-to-all-start.3 = ((bf16[64,144,128]{2,1,0:T(8,128)(2,1)}), bf16[64,144,128]{2,1,0:T(8,128)(2,1)S(1)}, u32[]{:S(2)}, u32[]{:S(2)}) async-start(bf16[64,144,128]{2,1,0:T(8,128)(2,1)} %add_convert_fusion), calls=%async_computation.3 | async-start | bytes 4718592 | tf_op jit(solution)/shard_map/all_to_all | solution.py:274
  183.2 65.2 %all-to-all-start.1 = ((bf16[64,144,128]{2,1,0:T(8,128)(2,1)}), bf16[64,144,128]{2,1,0:T(8,128)(2,1)}, u32[]{:S(2)}, u32[]{:S(2)}) async-start(bf16[64,144,128]{2,1,0:T(8,128)(2,1)} %add_convert_fusion.1), calls=%async_computation.1 | async-start | bytes 4718592 | tf_op jit(solution)/shard_map/all_to_all | solution.py:274
  192.6 1.5 copy-start.1
  195.1 2.3 collective-permute-start.4
  199.3 0.7 copy-start.2
  200.0 25.1 %collective-permute-start.5 = (bf16[16,32,128]{2,1,0:T(8,128)(2,1)}, bf16[16,32,128]{2,1,0:T(8,128)(2,1)S(1)}, u32[]{:S(2)}, u32[]{:S(2)}) collective-permute-start(bf16[16,32,128]{2,1,0:T(8,128)(2,1)} %get-tuple-element.27), channel_id=1, source_target_pairs={{0,32},{32,0},{64,96},{96,64},{1,33},{33,1},{65,97},{97,65},{2,34}... | collective-permute-start | bytes 393224 | tf_op jit(solution)/shard_map/ppermute | solution.py:312
  203.0 22.4 %collective-permute-start.6 = (bf16[16,32,128]{2,1,0:T(8,128)(2,1)}, bf16[16,32,128]{2,1,0:T(8,128)(2,1)S(1)}, u32[]{:S(2)}, u32[]{:S(2)}) collective-permute-start(bf16[16,32,128]{2,1,0:T(8,128)(2,1)} %get-tuple-element.28), channel_id=1, source_target_pairs={{0,64},{32,96},{64,0},{96,32},{1,65},{33,97},{65,1},{97,33},{2,66}... | collective-permute-start | bytes 393224 | tf_op jit(solution)/shard_map/ppermute | solution.py:312
  203.7 22.3 %collective-permute-start.7 = (bf16[16,32,128]{2,1,0:T(8,128)(2,1)S(1)}, bf16[16,32,128]{2,1,0:T(8,128)(2,1)S(1)}, u32[]{:S(2)}, u32[]{:S(2)}) collective-permute-start(bf16[16,32,128]{2,1,0:T(8,128)(2,1)S(1)} %get-tuple-element.29), channel_id=1, source_target_pairs={{0,96},{32,64},{64,32},{96,0},{1,97},{33,65},{65,33},{97,1},{2,98}... | collective-permute-start | bytes 393224 | tf_op jit(solution)/shard_map/ppermute | solution.py:312
  226.0 1.0 copy-start.3
  227.0 4.4 %collective-permute-start.10 = (f32[4,32,128]{2,1,0:T(8,128)S(1)}, f32[4,32,128]{2,1,0:T(8,128)S(1)}, u32[]{:S(2)}, u32[]{:S(2)}) collective-permute-start(f32[4,32,128]{2,1,0:T(8,128)S(1)} %get-tuple-element.33), channel_id=1, source_target_pairs={{0,24},{8,16},{16,8},{24,0},{1,25},{9,17},{17,9},{25,1},{2,26},{10... | collective-permute-start | bytes 196616 | tf_op jit(solution)/shard_map/ppermute | solution.py:312
  229.0 4.7 %collective-permute-start.8 = (f32[4,32,128]{2,1,0:T(8,128)S(1)}, f32[4,32,128]{2,1,0:T(8,128)S(1)}, u32[]{:S(2)}, u32[]{:S(2)}) collective-permute-start(f32[4,32,128]{2,1,0:T(8,128)S(1)} %get-tuple-element.31), channel_id=1, source_target_pairs={{0,8},{8,0},{16,24},{24,16},{1,9},{9,1},{17,25},{25,17},{2,10},{10... | collective-permute-start | bytes 196616 | tf_op jit(solution)/shard_map/ppermute | solution.py:312
  230.4 5.8 %collective-permute-start.9 = (f32[4,32,128]{2,1,0:T(8,128)S(1)}, f32[4,32,128]{2,1,0:T(8,128)S(1)}, u32[]{:S(2)}, u32[]{:S(2)}) collective-permute-start(f32[4,32,128]{2,1,0:T(8,128)S(1)} %get-tuple-element.32), channel_id=1, source_target_pairs={{0,16},{8,24},{16,0},{24,8},{1,17},{9,25},{17,1},{25,9},{2,18},{10... | collective-permute-start | bytes 196616 | tf_op jit(solution)/shard_map/ppermute | solution.py:312
  236.2 4.0 %collective-permute-start.11 = (f32[1,32,128]{2,1,0:T(8,128)S(1)}, f32[1,32,128]{2,1,0:T(8,128)S(1)}, u32[]{:S(2)}, u32[]{:S(2)}) collective-permute-start(f32[1,32,128]{2,1,0:T(8,128)S(1)} %get-tuple-element.35), channel_id=1, source_target_pairs={{0,2},{2,0},{4,6},{6,4},{1,3},{3,1},{5,7},{7,5},{8,10},{10,8},{12,... | collective-permute-start | bytes 49160 | tf_op jit(solution)/shard_map/ppermute | solution.py:312
  237.9 5.2 %collective-permute-start.12 = (f32[1,32,128]{2,1,0:T(8,128)S(1)}, f32[1,32,128]{2,1,0:T(8,128)S(1)}, u32[]{:S(2)}, u32[]{:S(2)}) collective-permute-start(f32[1,32,128]{2,1,0:T(8,128)S(1)} %get-tuple-element.36), channel_id=1, source_target_pairs={{0,4},{2,6},{4,0},{6,2},{1,5},{3,7},{5,1},{7,3},{8,12},{10,14},{12... | collective-permute-start | bytes 49160 | tf_op jit(solution)/shard_map/ppermute | solution.py:312
  240.1 3.7 %collective-permute-start.13 = (f32[1,32,128]{2,1,0:T(8,128)S(1)}, f32[1,32,128]{2,1,0:T(8,128)S(1)}, u32[]{:S(2)}, u32[]{:S(2)}) collective-permute-start(f32[1,32,128]{2,1,0:T(8,128)S(1)} %get-tuple-element.37), channel_id=1, source_target_pairs={{0,6},{2,4},{4,2},{6,0},{1,7},{3,5},{5,3},{7,1},{8,14},{10,12},{12... | collective-permute-start | bytes 49160 | tf_op jit(solution)/shard_map/ppermute | solution.py:312

commit v3 on v1

--- a/solution.py
+++ b/solution.py
@@ -107,10 +107,6 @@
     give_ref[:, 24:, :] = shared.astype(BF16)
 
 
-def spread(src_ref, flat_ref):
-    flat_ref.reshape(PAIRS, PITCH, 128)[:, :MSG, :] = src_ref[:, :MSG, :].astype(F32)
-
-
 def lay_out(flat_ref, rows_ref, first, last):
     for s in range(SLOTS):
         for j in range(first, last):
@@ -123,7 +119,7 @@
 
 def expert_kernel(
     core_ref, own_ref, other_ref, gate_ref, up_ref, down_ref, mine_ref, theirs_ref,
-    flats, rows, gate, up, down, acc, hid, w_ref, sem_g, sem_u, sem_d,
+    msgs, sem_m, flats, rows, gate, up, down, acc, hid, w_ref, sem_g, sem_u, sem_d,
 ):
     hidden = gate.shape[2]
 
@@ -139,14 +135,25 @@
         return pltpu.make_async_copy(up_ref.at[0, cut(k), :], up.at[slot], sem_u.at[slot])
 
     down_copy = pltpu.make_async_copy(down_ref.at[0], down, sem_d.at[0])
+    loads = [
+        pltpu.make_async_copy(in_ref.at[peers], msgs.at[side, peers], sem_m.at[side, i])
+        for side, in_ref in enumerate((own_ref,))
+        for i, peers in enumerate(CUTS)
+    ]
+    for load in loads:
+        load.start()
     for k in range(DEPTH - 1):
         gate_copy(k).start()
         up_copy(k).start()
     core = core_ref[0]
     lane = iota((PAIRS, 128), 1)
-    for side, in_ref in enumerate((own_ref, other_ref)):
+    for side in range(2):
         flat = flats.at[side]
-        spread(in_ref, flat)
+        for i, peers in enumerate(CUTS):
+            if side == 0:
+                loads[i].wait()
+            arrived = other_ref[peers] if side else msgs[side, peers]
+            flat.reshape(PAIRS, PITCH, 128)[peers, :MSG, :] = arrived.astype(F32)
         coef = flat[pl.ds(COEF_AT, PAIRS, stride=PITCH), :]
         for s in range(SLOTS):
             mine = jnp.where(lane // 2 == 2 * s + core, coef, 0.0)
@@ -189,8 +196,14 @@
         return carry
 
     lax.fori_loop(0, PIECES, columns, 0)
-    for side, out_ref in enumerate((mine_ref, theirs_ref)):
-        out_ref[...] = flats.at[side].reshape(PAIRS, PITCH, 128)[:, :MSG, :].astype(BF16)
+    saves = []
+    for side, out_ref in ((1, theirs_ref), (0, mine_ref)):
+        for i, peers in enumerate(CUTS):
+            msgs[side, peers] = flats.at[side].reshape(PAIRS, PITCH, 128)[peers, :MSG, :].astype(BF16)
+            saves.append(pltpu.make_async_copy(msgs.at[side, peers], out_ref.at[peers], sem_m.at[side, i]))
+            saves[-1].start()
+    for save in saves:
+        save.wait()
 
 
 def fold_kernel(place_ref, *refs):
@@ -205,16 +218,23 @@
         out_ref[...] = total_ref[pl.ds(at, size)].astype(out_ref.dtype)
 
 
-def mix_kernel(start, node_in, local_in, in_ref, *refs):
-    before, (out_ref, flat_ref, rows_ref, node_ref, local_ref, sum_ref, sem) = refs[:-7], refs[-7:]
-    copies = load_all([(node_in, node_ref), (local_in, local_ref)] + [(old, sum_ref) for old in before], sem)
+def mix_kernel(start, node_in, local_in, msg_in, *refs):
+    before, (out_ref, flat_ref, rows_ref, node_ref, local_ref, msg_ref, sum_ref, sem) = refs[:-8], refs[-8:]
+    loads = [(node_in, node_ref), (local_in, local_ref)]
+    if before:
+        loads += [(msg_in.at[cut], msg_ref.at[cut]) for cut in CUTS] + [(before[0], sum_ref)]
+    copies = load_all(loads, sem)
     copies[0].wait()
     copies[1].wait()
     pick = jnp.concatenate(picks(node_ref, local_ref, start), axis=0).astype(BF16)
-    spread(in_ref, flat_ref)
+    for i, cut in enumerate(CUTS):
+        if before:
+            copies[2 + i].wait()
+        arrived = msg_ref[cut] if before else msg_in[cut]
+        flat_ref.reshape(PAIRS, PITCH, 128)[cut, :MSG, :] = arrived.astype(F32)
     lay_out(flat_ref, rows_ref, 0, WIDE)
-    for copy in copies[2:]:
-        copy.wait()
+    if before:
+        copies[-1].wait()
     for k in range(7):
         at = slice(512 * k, 512 * (k + 1))
         value = lax.dot_general(pick, rows_ref[:, at], (((0,), (0,)), ((), ())), preferred_element_type=F32)
@@ -266,13 +286,15 @@
         )(*map(in_hbm, (*routes, affinity.T, tokens)))
 
     def experts(own, other):
-        shape = jax.ShapeDtypeStruct((PAIRS, MSG, 128), BF16)
+        shape = pltpu.HBM((PAIRS, MSG, 128), BF16)
         return pl.pallas_call(
             expert_kernel,
-            in_specs=[scalar, local, local] + [far] * 3,
-            out_specs=(local, local),
+            in_specs=[scalar, far, local] + [far] * 3,
+            out_specs=(far, far),
             out_shape=(shape, shape),
             scratch_shapes=[
+                pltpu.VMEM((2, PAIRS, MSG, 128), BF16),
+                dma((2, len(CUTS))),
                 pltpu.VMEM((2, PAIRS * PITCH, 128), F32),
                 pltpu.VMEM((2 * ROWS, width), BF16),
                 pltpu.VMEM((DEPTH, PIECE, hidden), BF16),
@@ -285,12 +307,12 @@
                 dma((DEPTH,)),
                 dma((1,)),
             ],
-            compiler_params=vmem(46),
+            compiler_params=vmem(50),
             cost_estimate=pl.CostEstimate(
                 flops=12 * ROWS * width * hidden, bytes_accessed=6 * width * hidden + 16 * ROWS * width, transcendentals=0
             ),
             name="experts",
-        )(core, own, other, *map(in_hbm, (w_gate, w_up, w_down)))
+        )(core, in_hbm(own), other, *map(in_hbm, (w_gate, w_up, w_down)))
 
     def pair_result(message):
         other = lax.ppermute(message, "core", swap)
@@ -317,14 +339,14 @@
     def mix(start, message, *before):
         return pl.pallas_call(
             functools.partial(mix_kernel, start),
-            in_specs=[far, far, local] + [far] * len(before),
+            in_specs=[far, far] + ([far, far] if before else [local]),
             out_shape=jax.ShapeDtypeStruct((tok, width), BF16) if before else pltpu.HBM((tok, width), F32),
             scratch_shapes=[flat, rows]
             + small
-            + [pltpu.VMEM((tok, width), F32), dma((3,))],
+            + [pltpu.VMEM((PAIRS, MSG, 128), BF16), pltpu.VMEM((tok, width), F32), dma((7,))],
             compiler_params=vmem(32),
             name="mix",
-        )(*map(in_hbm, routes), message, *map(in_hbm, before))
+        )(*map(in_hbm, routes), in_hbm(message) if before else message, *map(in_hbm, before))
 
     halves = pl.pallas_call(
         halves_kernel,

time: 256 us -> 259 us (1.012)
  Pallas kernels: 67.4 us -> 71.6 us
    pallas_call x4, Pallas kernels: 56.7 us -> 60.9 us  [the longest x2 52.7 us: experts(): pl.pallas_call(expert_kernel, in_specs=[scalar, far, local] + [far] * 3,...]
  transfers between devices with their start and end apart: 16 -> 16, of which waited for: 10 -> 10; matrix products, arithmetic and copies ran while one was open for 3% -> 3% of each run, Pallas kernels for 22% -> 23%
where the time goes in v3:
time: 259 us; the launch traced here: 255 us
  blocking collectives  82.1 us (32%)
  Pallas kernels  71.6 us (28%)
  waiting for transfers between devices  60 us (23%)
  starting transfers between devices  30.2 us (12%)
  other arithmetic  7.09 us (3%)
  local copies, waits for them, and re-layouts  3.16 us (1%)
    all_to_all x2, blocking collectives, exchange(): lax.all_to_all(message, chips, split_axis=0, concat_axis=0, tiled=True)  82.1 us
    pallas_call x2, Pallas kernels, experts(): pl.pallas_call(expert_kernel, in_specs=[scalar, far, local] + [far] * 3,...  52.7 us
    ppermute x9, waiting for transfers between devices, fold(): lax.ppermute(part, axes, [(i, i ^ flip) for i in range(4)])  30.9 us
    all_to_all x2, waiting for transfers between devices, exchange(): lax.all_to_all(message, chips, split_axis=0, concat_axis=0, tiled=True)  26.8 us
    all_to_all x2, starting transfers between devices, exchange(): lax.all_to_all(message, chips, split_axis=0, concat_axis=0, tiled=True)  17.1 us
    ppermute x9, starting transfers between devices, fold(): lax.ppermute(part, axes, [(i, i ^ flip) for i in range(4)])  12.1 us
    pallas_call x2, Pallas kernels, mix(): pl.pallas_call(functools.partial(mix_kernel, start), in_specs=[far, far]...  8.15 us
    pallas_call x2, Pallas kernels, send(): pl.pallas_call(functools.partial(send_kernel, start), in_specs=[far] * 4,...  7.73 us
  transfers between devices with their start and end apart: 16, of which 10 were waited for; matrix products, arithmetic and copies ran while one was open for 3% of the time, Pallas kernels for 23%

profile of v3, /device:TPU:10, one launch (start us, length us, event | category | flops | bytes accessed | tf_op | source)
XLA Modules:
  0.0 255.1 jit_solution(17993459040315839789)
XLA Ops:
  0.6 3.9 %send.3 = bf16[64,144,128]{2,1,0:T(8,128)(2,1)} custom-call(s32[4,128]{1,0:T(4,128)} %bitcast.21, s32[8,128]{1,0:T(8,128)} %bitcast.17, f32[8,128]{1,0:T(8,128)} %bitcast.25, bf16[128,3584]{1,0:T(8,128)(2,1)} %tok_in.3), custom_call_target="tpu_custom_call" | custom-call | tf_op jit(solution)/shard_map/send/pallas_call | solution.py:276
  4.5 42.6 %all_to_all.20.own_ref = bf16[64,144,128]{2,1,0:T(8,128)(2,1)} all-to-all(bf16[64,144,128]{2,1,0:T(8,128)(2,1)} %send.3), channel_id=1, replica_groups=mesh['edp'=2,'zh'=2,'x'=4,'y'=4,'core'=2] {'edp','zh','x','y'}, dimensions={0} | all-to-all | bytes 4718592 | tf_op jit(solution)/shard_map/all_to_all | solution.py:272
  47.1 0.0 collective-permute-start.2
  47.2 3.9 %send.2 = bf16[64,144,128]{2,1,0:T(8,128)(2,1)} custom-call(s32[4,128]{1,0:T(4,128)} %bitcast.22, s32[8,128]{1,0:T(8,128)} %bitcast.18, f32[8,128]{1,0:T(8,128)} %bitcast.26, bf16[128,3584]{1,0:T(8,128)(2,1)} %tok_in.3), custom_call_target="tpu_custom_call" | custom-call | tf_op jit(solution)/shard_map/send/pallas_call | solution.py:276
  51.0 39.5 %all_to_all.21.own_ref = bf16[64,144,128]{2,1,0:T(8,128)(2,1)} all-to-all(bf16[64,144,128]{2,1,0:T(8,128)(2,1)} %send.2), channel_id=1, replica_groups=mesh['edp'=2,'zh'=2,'x'=4,'y'=4,'core'=2] {'edp','zh','x','y'}, dimensions={0} | all-to-all | bytes 4718592 | tf_op jit(solution)/shard_map/all_to_all | solution.py:272
  90.5 0.0 collective-permute-start
  90.5 0.0 collective-permute-done.2.other_ref
  90.5 27.2 %experts.3 = (bf16[64,144,128]{2,1,0:T(8,128)(2,1)}, bf16[64,144,128]{2,1,0:T(8,128)(2,1)}) custom-call(s32[1]{0:T(128)} %bitcast.2.core_ref, bf16[64,144,128]{2,1,0:T(8,128)(2,1)} %all_to_all.20.own_ref, bf16[64,144,128]{2,1,0:T(8,128)(2,1)} %collective-permute-done.2.other_ref, bf16[1,3584,1024]{2,1,0:T(8,128)(2,1)} %gate_ref.3, ...), custom_call_target="tpu_custom_call" | custom-call | flops 14092861440 | bytes 40370176 | tf_op jit(solution)/shard_map/experts/pallas_call | solution.py:290
  117.7 0.0 copy-start.3
  117.7 0.8 collective-permute-start.3
  118.5 0.0 collective-permute-done.other_ref
  118.5 25.5 %experts.2 = (bf16[64,144,128]{2,1,0:T(8,128)(2,1)}, bf16[64,144,128]{2,1,0:T(8,128)(2,1)}) custom-call(s32[1]{0:T(128)} %bitcast.2.core_ref, bf16[64,144,128]{2,1,0:T(8,128)(2,1)} %all_to_all.21.own_ref, bf16[64,144,128]{2,1,0:T(8,128)(2,1)S(1)} %collective-permute-done.other_ref, bf16[1,3584,1024]{2,1,0:T(8,128)(2,1)} %gate_ref.3, ...), custom_call_target="tpu_custom_call" | custom-call | flops 14092861440 | bytes 40370176 | tf_op jit(solution)/shard_map/experts/pallas_call | solution.py:290
  144.0 0.2 collective-permute-start.1
  144.3 0.0 collective-permute-done.3
  144.3 0.0 copy-done.3
  144.3 2.0 add_convert_fusion
  146.3 7.9 %all-to-all-start.3 = ((bf16[64,144,128]{2,1,0:T(8,128)(2,1)}), bf16[64,144,128]{2,1,0:T(8,128)(2,1)S(1)}, u32[]{:S(2)}, u32[]{:S(2)}) async-start(bf16[64,144,128]{2,1,0:T(8,128)(2,1)} %add_convert_fusion), calls=%async_computation.3 | async-start | bytes 4718592 | tf_op jit(solution)/shard_map/all_to_all | solution.py:272
  154.3 0.0 collective-permute-done.1
  154.3 4.4 %add_convert_fusion.1 = bf16[64,144,128]{2,1,0:T(8,128)(2,1)} fusion(bf16[64,144,128]{2,1,0:T(8,128)(2,1)} %collective-permute-done.1, bf16[64,144,128]{2,1,0:T(8,128)(2,1)} %get-tuple-element.20), kind=kLoop, calls=%fused_computation.1 | loop fusion | flops 4718592 | bytes 7077888 | tf_op jit(solution)/shard_map/convert_element_type | solution.py:321
  158.7 26.8 %all-to-all-done.3.msg_in = bf16[64,144,128]{2,1,0:T(8,128)(2,1)S(1)} async-done(((bf16[64,144,128]{2,1,0:T(8,128)(2,1)}), bf16[64,144,128]{2,1,0:T(8,128)(2,1)S(1)}, u32[]{:S(2)}, u32[]{:S(2)}) %all-to-all-start.3) | async-done | bytes 2359328 | tf_op jit(solution)/shard_map/all_to_all | solution.py:272
  185.5 9.2 %all-to-all-start.1 = ((bf16[64,144,128]{2,1,0:T(8,128)(2,1)}), bf16[64,144,128]{2,1,0:T(8,128)(2,1)}, u32[]{:S(2)}, u32[]{:S(2)}) async-start(bf16[64,144,128]{2,1,0:T(8,128)(2,1)} %add_convert_fusion.1), calls=%async_computation.1 | async-start | bytes 4718592 | tf_op jit(solution)/shard_map/all_to_all | solution.py:272
  194.7 0.0 copy-start
  194.7 1.5 copy-done
  196.2 1.0 halves.1
  197.2 0.0 collective-permute-start.4
  197.2 2.2 collective-permute-done.4.refs_1_
  199.4 1.9 fold.3
  201.3 0.0 copy-start.1
  201.3 0.7 copy-done.1
  202.0 3.0 %collective-permute-start.5 = (bf16[16,32,128]{2,1,0:T(8,128)(2,1)}, bf16[16,32,128]{2,1,0:T(8,128)(2,1)S(1)}, u32[]{:S(2)}, u32[]{:S(2)}) collective-permute-start(bf16[16,32,128]{2,1,0:T(8,128)(2,1)} %get-tuple-element.27), channel_id=1, source_target_pairs={{0,32},{32,0},{64,96},{96,64},{1,33},{33,1},{65,97},{97,65},{2,34}... | collective-permute-start | bytes 393224 | tf_op jit(solution)/shard_map/ppermute | solution.py:336
  205.0 0.8 collective-permute-start.6
  205.8 0.5 collective-permute-start.7
  206.3 20.7 %collective-permute-done.5.refs_1_ = bf16[16,32,128]{2,1,0:T(8,128)(2,1)S(1)} collective-permute-done((bf16[16,32,128]{2,1,0:T(8,128)(2,1)}, bf16[16,32,128]{2,1,0:T(8,128)(2,1)S(1)}, u32[]{:S(2)}, u32[]{:S(2)}) %collective-permute-start.5) | collective-permute-done | bytes 131104 | tf_op jit(solution)/shard_map/ppermute | solution.py:336
  227.0 0.2 collective-permute-done.6.refs_2_
  227.2 0.8 collective-permute-done.7.refs_3_
  228.0 0.0 copy-start.2
  228.0 0.9 copy-done.2
  228.9 0.1 fold.4
  229.0 1.9 collective-permute-start.10
  230.9 1.4 collective-permute-start.8
  232.4 0.2 collective-permute-start.9
  232.6 0.8 collective-permute-done.10.refs_3_
  233.3 2.4 collective-permute-done.8.refs_1_
  235.8 2.4 collective-permute-done.9.refs_2_
  238.2 2.2 collective-permute-start.11
  240.3 2.1 collective-permute-start.12
  242.4 0.0 collective-permute-start.13
  242.4 0.0 collective-permute-done.11
  242.4 3.2 %collective-permute-done.12 = f32[1,32,128]{2,1,0:T(8,128)S(1)} collective-permute-done((f32[1,32,128]{2,1,0:T(8,128)S(1)}, f32[1,32,128]{2,1,0:T(8,128)S(1)}, u32[]{:S(2)}, u32[]{:S(2)}) %collective-permute-start.12) | collective-permute-done | bytes 16416 | tf_op jit(solution)/shard_map/ppermute | solution.py:336
  245.6 0.6 collective-permute-done.13
  246.2 0.6 fusion
  246.8 3.9 %mix.2.refs_0_ = f32[128,3584]{1,0:T(8,128)} custom-call(s32[4,128]{1,0:T(4,128)} %bitcast.23, s32[8,128]{1,0:T(8,128)} %bitcast.19, bf16[64,144,128]{2,1,0:T(8,128)(2,1)S(1)} %all-to-all-done.3.msg_in), custom_call_target="tpu_custom_call" | custom-call | tf_op jit(solution)/shard_map/mix/pallas_call | solution.py:340
  250.7 0.0 all-to-all-done.1.msg_in
  250.7 4.2 %mix.3 = bf16[128,3584]{1,0:T(8,128)(2,1)} custom-call(s32[4,128]{1,0:T(4,128)} %bitcast.24, s32[8,128]{1,0:T(8,128)} %bitcast.20, bf16[64,144,128]{2,1,0:T(8,128)(2,1)} %all-to-all-done.1.msg_in, f32[128,3584]{1,0:T(8,128)} %mix.2.refs_0_), custom_call_target="tpu_custom_call" | custom-call | tf_op jit(solution)/shard_map/mix/pallas_call | solution.py:340
  (4 shorter events, 0.0 us)
Async XLA Ops:
  47.1 43.4 %collective-permute-start.2 = (bf16[64,144,128]{2,1,0:T(8,128)(2,1)}, bf16[64,144,128]{2,1,0:T(8,128)(2,1)}, u32[]{:S(2)}, u32[]{:S(2)}) collective-permute-start(bf16[64,144,128]{2,1,0:T(8,128)(2,1)} %all_to_all.20.own_ref), channel_id=1, source_target_pairs={{0,1},{1,0},{2,3},{3,2},{4,5},{5,4},{6,7},{7,6},{8,9},{9,8},{10,11... | collective-permute-start | bytes 7077896 | tf_op jit(solution)/shard_map/ppermute | solution.py:318
  90.5 28.0 %collective-permute-start = (bf16[64,144,128]{2,1,0:T(8,128)(2,1)}, bf16[64,144,128]{2,1,0:T(8,128)(2,1)S(1)}, u32[]{:S(2)}, u32[]{:S(2)}) collective-permute-start(bf16[64,144,128]{2,1,0:T(8,128)(2,1)} %all_to_all.21.own_ref), channel_id=1, source_target_pairs={{0,1},{1,0},{2,3},{3,2},{4,5},{5,4},{6,7},{7,6},{8,9},{9,8},{10,11... | collective-permute-start | bytes 7077896 | tf_op jit(solution)/shard_map/ppermute | solution.py:318
  117.7 26.5 %copy-start.3 = (bf16[64,144,128]{2,1,0:T(8,128)(2,1)S(1)}, bf16[64,144,128]{2,1,0:T(8,128)(2,1)}, u32[]{:S(2)}) copy-start(bf16[64,144,128]{2,1,0:T(8,128)(2,1)} %get-tuple-element.22) | copy-start | bytes 7077892
  117.7 26.5 %collective-permute-start.3 = (bf16[64,144,128]{2,1,0:T(8,128)(2,1)}, bf16[64,144,128]{2,1,0:T(8,128)(2,1)S(1)}, u32[]{:S(2)}, u32[]{:S(2)}) collective-permute-start(bf16[64,144,128]{2,1,0:T(8,128)(2,1)} %get-tuple-element.23), channel_id=1, source_target_pairs={{0,1},{1,0},{2,3},{3,2},{4,5},{5,4},{6,7},{7,6},{8,9},{9,8},{10,11... | collective-permute-start | bytes 7077896 | tf_op jit(solution)/shard_map/ppermute | solution.py:320
  144.0 10.2 %collective-permute-start.1 = (bf16[64,144,128]{2,1,0:T(8,128)(2,1)}, bf16[64,144,128]{2,1,0:T(8,128)(2,1)}, u32[]{:S(2)}, u32[]{:S(2)}) collective-permute-start(bf16[64,144,128]{2,1,0:T(8,128)(2,1)} %get-tuple-element.21), channel_id=1, source_target_pairs={{0,1},{1,0},{2,3},{3,2},{4,5},{5,4},{6,7},{7,6},{8,9},{9,8},{10,11... | collective-permute-start | bytes 7077896 | tf_op jit(solution)/shard_map/ppermute | solution.py:320
  146.3 39.2 %all-to-all-start.3 = ((bf16[64,144,128]{2,1,0:T(8,128)(2,1)}), bf16[64,144,128]{2,1,0:T(8,128)(2,1)S(1)}, u32[]{:S(2)}, u32[]{:S(2)}) async-start(bf16[64,144,128]{2,1,0:T(8,128)(2,1)} %add_convert_fusion), calls=%async_computation.3 | async-start | bytes 4718592 | tf_op jit(solution)/shard_map/all_to_all | solution.py:272
  185.5 65.2 %all-to-all-start.1 = ((bf16[64,144,128]{2,1,0:T(8,128)(2,1)}), bf16[64,144,128]{2,1,0:T(8,128)(2,1)}, u32[]{:S(2)}, u32[]{:S(2)}) async-start(bf16[64,144,128]{2,1,0:T(8,128)(2,1)} %add_convert_fusion.1), calls=%async_computation.1 | async-start | bytes 4718592 | tf_op jit(solution)/shard_map/all_to_all | solution.py:272
  194.7 1.5 copy-start
  197.2 2.3 collective-permute-start.4
  201.3 0.7 copy-start.1
  202.0 25.0 %collective-permute-start.5 = (bf16[16,32,128]{2,1,0:T(8,128)(2,1)}, bf16[16,32,128]{2,1,0:T(8,128)(2,1)S(1)}, u32[]{:S(2)}, u32[]{:S(2)}) collective-permute-start(bf16[16,32,128]{2,1,0:T(8,128)(2,1)} %get-tuple-element.27), channel_id=1, source_target_pairs={{0,32},{32,0},{64,96},{96,64},{1,33},{33,1},{65,97},{97,65},{2,34}... | collective-permute-start | bytes 393224 | tf_op jit(solution)/shard_map/ppermute | solution.py:336
  205.0 22.1 %collective-permute-start.6 = (bf16[16,32,128]{2,1,0:T(8,128)(2,1)}, bf16[16,32,128]{2,1,0:T(8,128)(2,1)S(1)}, u32[]{:S(2)}, u32[]{:S(2)}) collective-permute-start(bf16[16,32,128]{2,1,0:T(8,128)(2,1)} %get-tuple-element.28), channel_id=1, source_target_pairs={{0,64},{32,96},{64,0},{96,32},{1,65},{33,97},{65,1},{97,33},{2,66}... | collective-permute-start | bytes 393224 | tf_op jit(solution)/shard_map/ppermute | solution.py:336
  205.8 22.1 %collective-permute-start.7 = (bf16[16,32,128]{2,1,0:T(8,128)(2,1)S(1)}, bf16[16,32,128]{2,1,0:T(8,128)(2,1)S(1)}, u32[]{:S(2)}, u32[]{:S(2)}) collective-permute-start(bf16[16,32,128]{2,1,0:T(8,128)(2,1)S(1)} %get-tuple-element.29), channel_id=1, source_target_pairs={{0,96},{32,64},{64,32},{96,0},{1,97},{33,65},{65,33},{97,1},{2,98}... | collective-permute-start | bytes 393224 | tf_op jit(solution)/shard_map/ppermute | solution.py:336
  228.0 1.0 copy-start.2
  229.0 4.3 %collective-permute-start.10 = (f32[4,32,128]{2,1,0:T(8,128)S(1)}, f32[4,32,128]{2,1,0:T(8,128)S(1)}, u32[]{:S(2)}, u32[]{:S(2)}) collective-permute-start(f32[4,32,128]{2,1,0:T(8,128)S(1)} %get-tuple-element.33), channel_id=1, source_target_pairs={{0,24},{8,16},{16,8},{24,0},{1,25},{9,17},{17,9},{25,1},{2,26},{10... | collective-permute-start | bytes 196616 | tf_op jit(solution)/shard_map/ppermute | solution.py:336
  230.9 4.8 %collective-permute-start.8 = (f32[4,32,128]{2,1,0:T(8,128)S(1)}, f32[4,32,128]{2,1,0:T(8,128)S(1)}, u32[]{:S(2)}, u32[]{:S(2)}) collective-permute-start(f32[4,32,128]{2,1,0:T(8,128)S(1)} %get-tuple-element.31), channel_id=1, source_target_pairs={{0,8},{8,0},{16,24},{24,16},{1,9},{9,1},{17,25},{25,17},{2,10},{10... | collective-permute-start | bytes 196616 | tf_op jit(solution)/shard_map/ppermute | solution.py:336
  232.4 5.8 %collective-permute-start.9 = (f32[4,32,128]{2,1,0:T(8,128)S(1)}, f32[4,32,128]{2,1,0:T(8,128)S(1)}, u32[]{:S(2)}, u32[]{:S(2)}) collective-permute-start(f32[4,32,128]{2,1,0:T(8,128)S(1)} %get-tuple-element.32), channel_id=1, source_target_pairs={{0,16},{8,24},{16,0},{24,8},{1,17},{9,25},{17,1},{25,9},{2,18},{10... | collective-permute-start | bytes 196616 | tf_op jit(solution)/shard_map/ppermute | solution.py:336
  238.2 4.3 %collective-permute-start.11 = (f32[1,32,128]{2,1,0:T(8,128)S(1)}, f32[1,32,128]{2,1,0:T(8,128)S(1)}, u32[]{:S(2)}, u32[]{:S(2)}) collective-permute-start(f32[1,32,128]{2,1,0:T(8,128)S(1)} %get-tuple-element.35), channel_id=1, source_target_pairs={{0,2},{2,0},{4,6},{6,4},{1,3},{3,1},{5,7},{7,5},{8,10},{10,8},{12,... | collective-permute-start | bytes 49160 | tf_op jit(solution)/shard_map/ppermute | solution.py:336
  240.3 5.2 %collective-permute-start.12 = (f32[1,32,128]{2,1,0:T(8,128)S(1)}, f32[1,32,128]{2,1,0:T(8,128)S(1)}, u32[]{:S(2)}, u32[]{:S(2)}) collective-permute-start(f32[1,32,128]{2,1,0:T(8,128)S(1)} %get-tuple-element.36), channel_id=1, source_target_pairs={{0,4},{2,6},{4,0},{6,2},{1,5},{3,7},{5,1},{7,3},{8,12},{10,14},{12... | collective-permute-start | bytes 49160 | tf_op jit(solution)/shard_map/ppermute | solution.py:336
  242.4 3.7 %collective-permute-start.13 = (f32[1,32,128]{2,1,0:T(8,128)S(1)}, f32[1,32,128]{2,1,0:T(8,128)S(1)}, u32[]{:S(2)}, u32[]{:S(2)}) collective-permute-start(f32[1,32,128]{2,1,0:T(8,128)S(1)} %get-tuple-element.37), channel_id=1, source_target_pairs={{0,6},{2,4},{4,2},{6,0},{1,7},{3,5},{5,3},{7,1},{8,14},{10,12},{12... | collective-permute-start | bytes 49160 | tf_op jit(solution)/shard_map/ppermute | solution.py:336

commit v4 on v1

--- a/solution.py
+++ b/solution.py
@@ -48,9 +48,8 @@
     return copies
 
 
-def send_kernel(
-    start, node_in, local_in, aff_in, tok_in, out_ref, flat_ref, stage_ref, node_ref, local_ref, aff_ref, tok_ref, sem
-):
+def send_kernel(start, node_in, local_in, aff_in, tok_in, *refs):
+    grad_refs, (out_ref, flat_ref, stage_ref, node_ref, local_ref, aff_ref, tok_ref, sem) = refs[:-8], refs[-8:]
     here = ((node_in, node_ref), (local_in, local_ref), (aff_in, aff_ref), (tok_in, tok_ref))
     copies = load_all(here, sem)
     for copy in copies[:3]:
@@ -89,7 +88,10 @@
         flat_ref[pl.ds(row, PAIRS, stride=PITCH), :] = coef
     saves = []
     for i, cut in enumerate(CUTS):
-        stage_ref[cut] = flat_ref.reshape(PAIRS, PITCH, 128)[cut, :MSG, :].astype(BF16)
+        stage_ref[cut, :MSG, :] = flat_ref.reshape(PAIRS, PITCH, 128)[cut, :MSG, :].astype(BF16)
+        if grad_refs:
+            keep_ref, got_ref = grad_refs
+            stage_ref[cut, MSG:, :] = (keep_ref[cut] + got_ref[cut].astype(F32)).astype(BF16)
         saves.append(pltpu.make_async_copy(stage_ref.at[cut], out_ref.at[cut], sem.at[4 + i]))
         saves[-1].start()
     for save in saves:
@@ -193,28 +195,23 @@
         out_ref[...] = flats.at[side].reshape(PAIRS, PITCH, 128)[:, :MSG, :].astype(BF16)
 
 
-def fold_kernel(place_ref, *refs):
-    parts, (total_ref, outs) = refs[:-5], (refs[-1], refs[-5:-1])
-    total = parts[0][...].astype(F32)
-    for part in parts[1:]:
-        total = total + part[...].astype(F32)
-    total_ref[...] = total
-    size = total_ref.shape[0] // 4
-    for flip, out_ref in enumerate(outs):
-        at = jnp.bitwise_xor(place_ref[0], flip) * size
-        out_ref[...] = total_ref[pl.ds(at, size)].astype(out_ref.dtype)
-
-
-def mix_kernel(start, node_in, local_in, in_ref, *refs):
-    before, (out_ref, flat_ref, rows_ref, node_ref, local_ref, sum_ref, sem) = refs[:-7], refs[-7:]
-    copies = load_all([(node_in, node_ref), (local_in, local_ref)] + [(old, sum_ref) for old in before], sem)
+def mix_kernel(start, node_in, local_in, msg_in, *refs):
+    before, (out_ref, flat_ref, rows_ref, node_ref, local_ref, msg_ref, sum_ref, sem) = refs[:-8], refs[-8:]
+    loads = [(node_in, node_ref), (local_in, local_ref)]
+    if before:
+        loads += [(msg_in.at[cut], msg_ref.at[cut]) for cut in CUTS] + [(before[0], sum_ref)]
+    copies = load_all(loads, sem)
     copies[0].wait()
     copies[1].wait()
     pick = jnp.concatenate(picks(node_ref, local_ref, start), axis=0).astype(BF16)
-    spread(in_ref, flat_ref)
+    for i, cut in enumerate(CUTS):
+        if before:
+            copies[2 + i].wait()
+        arrived = msg_ref[cut] if before else msg_in[cut]
+        flat_ref.reshape(PAIRS, PITCH, 128)[cut, :MSG, :] = arrived.astype(F32)
     lay_out(flat_ref, rows_ref, 0, WIDE)
-    for copy in copies[2:]:
-        copy.wait()
+    if before:
+        copies[-1].wait()
     for k in range(7):
         at = slice(512 * k, 512 * (k + 1))
         value = lax.dot_general(pick, rows_ref[:, at], (((0,), (0,)), ((), ())), preferred_element_type=F32)
@@ -251,11 +248,11 @@
     def exchange(message):
         return lax.all_to_all(message, chips, split_axis=0, concat_axis=0, tiled=True)
 
-    def send(start):
-        shape = (PAIRS, MSG, 128)
+    def send(start, *grads):
+        shape = (PAIRS, MSG + (GRAD if grads else 0), 128)
         return pl.pallas_call(
             functools.partial(send_kernel, start),
-            in_specs=[far] * 4,
+            in_specs=[far] * 4 + [local] * len(grads),
             out_specs=far,
             out_shape=pltpu.HBM(shape, BF16),
             scratch_shapes=[flat, pltpu.VMEM(shape, BF16)]
@@ -263,7 +260,7 @@
             + [pltpu.VMEM((8, tok), F32), pltpu.VMEM((tok, width), BF16), dma((8,))],
             compiler_params=vmem(32),
             name="send",
-        )(*map(in_hbm, (*routes, affinity.T, tokens)))
+        )(*map(in_hbm, (*routes, affinity.T, tokens)), *grads)
 
     def experts(own, other):
         shape = jax.ShapeDtypeStruct((PAIRS, MSG, 128), BF16)
@@ -298,33 +295,17 @@
         back = lax.ppermute(theirs, "core", swap)
         return (mine.astype(F32) + back.astype(F32)).astype(BF16)
 
-    def fold(axes, dtype, *parts):
-        size = parts[0].shape[0] // 4
-        shapes = [jax.ShapeDtypeStruct((size, GRAD, 128), F32)] + [jax.ShapeDtypeStruct((size, GRAD, 128), dtype)] * 3
-        kept, *given = pl.pallas_call(
-            fold_kernel,
-            in_specs=[scalar] + [local] * len(parts),
-            out_specs=[local] * 4,
-            out_shape=shapes,
-            scratch_shapes=[pltpu.VMEM(parts[0].shape, F32)],
-            compiler_params=vmem(16),
-            name="fold",
-        )(place(axes), *parts)
-        return [kept] + [
-            lax.ppermute(part, axes, [(i, i ^ flip) for i in range(4)]) for flip, part in enumerate(given, 1)
-        ]
-
     def mix(start, message, *before):
         return pl.pallas_call(
             functools.partial(mix_kernel, start),
-            in_specs=[far, far, local] + [far] * len(before),
+            in_specs=[far, far] + ([far, far] if before else [local]),
             out_shape=jax.ShapeDtypeStruct((tok, width), BF16) if before else pltpu.HBM((tok, width), F32),
             scratch_shapes=[flat, rows]
             + small
-            + [pltpu.VMEM((tok, width), F32), dma((3,))],
+            + [pltpu.VMEM((PAIRS, MSG, 128), BF16), pltpu.VMEM((tok, width), F32), dma((7,))],
             compiler_params=vmem(32),
             name="mix",
-        )(*map(in_hbm, routes), message, *map(in_hbm, before))
+        )(*map(in_hbm, routes), in_hbm(message) if before else message, *map(in_hbm, before))
 
     halves = pl.pallas_call(
         halves_kernel,
@@ -338,23 +319,19 @@
     )
     keep, give = halves(core, grad_parts[0])
     got = lax.ppermute(give, "core", swap)
-    parts = fold(("edp", "zh"), BF16, keep, got)
-    parts = fold("x", F32, *parts)
-    parts = fold("y", F32, *parts)
-    total = (parts[0] + parts[1] + parts[2] + parts[3])[0]
-    low = total[:WIDE]
-    high = jnp.concatenate([total[WIDE:], total[:24]], axis=0)
-    router_grad = jnp.where(core[0] == 0, low, high)
     message = send(0)
     arrived = exchange(message)
-    message_2 = send(SLOTS)
+    message_2 = send(SLOTS, keep, got)
     arrived_2 = exchange(message_2)
     result = pair_result(arrived)
     returned = exchange(result)
     result_2 = pair_result(arrived_2)
     returned_2 = exchange(result_2)
     partial = mix(0, returned)
-    return mix(SLOTS, returned_2, partial), router_grad
+    mixed = mix(SLOTS, returned_2, partial)
+    total = jnp.sum(arrived_2[:, MSG:, :].astype(F32), axis=0)
+    high = jnp.concatenate([total[WIDE:], total[:24]], axis=0)
+    return mixed, jnp.where(core[0] == 0, total[:WIDE], high)
 
 
 def solution(mesh):

time: 256 us -> 233 us (0.910)
  blocking collectives: 82 us -> 0 us
  waiting for transfers between devices: 60.4 us -> 110 us
  starting transfers between devices: 30.2 us -> 39 us
  Pallas kernels: 67.4 us -> 63.2 us
  local copies, waits for them, and re-layouts: 4.58 us -> 8.69 us
    all_to_all x2 -> x0, blocking collectives: 82 us -> none  [exchange(): lax.all_to_all(message, chips, split_axis=0, concat_axis=0, tiled=True)]
    all_to_all x2 -> x4, waiting for transfers between devices: 27 us -> 108 us  [exchange(): lax.all_to_all(message, chips, split_axis=0, concat_axis=0, tiled=True)]
    ppermute x9 -> x0, waiting for transfers between devices: 31.1 us -> none  [fold(): lax.ppermute(part, axes, [(i, i ^ flip) for i in range(4)])]
    all_to_all x2 -> x4, starting transfers between devices: 17.4 us -> 38.1 us  [exchange(): lax.all_to_all(message, chips, split_axis=0, concat_axis=0, tiled=True)]
    ppermute x9 -> x0, starting transfers between devices: 12 us -> none  [fold(): lax.ppermute(part, axes, [(i, i ^ flip) for i in range(4)])]
    unnamed x8 -> x12, local copies, waits for them, and re-layouts: 4.57 us -> 8.69 us
    pallas_call x7 -> x4, Pallas kernels: 18.8 us -> 16 us  [the longest x2 8.08 us: mix(): pl.pallas_call(functools.partial(mix_kernel, start), in_specs=[far, far]...]
  transfers between devices with their start and end apart: 16 -> 9, of which waited for: 10 -> 5; matrix products, arithmetic and copies ran while one was open for 3% -> 4% of each run, Pallas kernels for 22% -> 22%
where the time goes in v4:
time: 233 us; the launch traced here: 230 us
  waiting for transfers between devices  110 us (47%)
  Pallas kernels  63.2 us (27%)
  starting transfers between devices  39 us (17%)
  local copies, waits for them, and re-layouts  8.69 us (4%)
  other arithmetic  8.3 us (4%)
    all_to_all x4, waiting for transfers between devices, exchange(): lax.all_to_all(message, chips, split_axis=0, concat_axis=0, tiled=True)  108 us
    pallas_call x2, Pallas kernels, experts(): pl.pallas_call(expert_kernel, in_specs=[scalar, local, local] + [far] * 3...  47 us
    all_to_all x4, starting transfers between devices, exchange(): lax.all_to_all(message, chips, split_axis=0, concat_axis=0, tiled=True)  38.1 us
    unnamed x12, local copies, waits for them, and re-layouts  8.69 us
    pallas_call x2, Pallas kernels, mix(): pl.pallas_call(functools.partial(mix_kernel, start), in_specs=[far, far]...  8.08 us
    pallas_call x2, Pallas kernels, send(): pl.pallas_call(functools.partial(send_kernel, start), in_specs=[far] * 4...  7.93 us
    convert_element_type x2, other arithmetic, pair_result(): return (mine.astype(F32) + back.astype(F32)).astype(BF16)  6.53 us
  transfers between devices with their start and end apart: 9, of which 5 were waited for; matrix products, arithmetic and copies ran while one was open for 4% of the time, Pallas kernels for 22%

profile of v4, /device:TPU:10, one launch (start us, length us, event | category | flops | bytes accessed | tf_op | source)
XLA Modules:
  0.0 229.9 jit_solution(7482973037789126076)
XLA Ops:
  0.6 3.9 %send.3 = bf16[64,144,128]{2,1,0:T(8,128)(2,1)} custom-call(s32[4,128]{1,0:T(4,128)} %bitcast.10, s32[8,128]{1,0:T(8,128)} %bitcast.6, f32[8,128]{1,0:T(8,128)} %bitcast.14, bf16[128,3584]{1,0:T(8,128)(2,1)} %tok_in.3), custom_call_target="tpu_custom_call" | custom-call | tf_op jit(solution)/shard_map/send/pallas_call | solution.py:253
  4.5 11.4 %all-to-all-start.2 = ((bf16[64,144,128]{2,1,0:T(8,128)(2,1)}), bf16[64,144,128]{2,1,0:T(8,128)(2,1)S(1)}, u32[]{:S(2)}, u32[]{:S(2)}) async-start(bf16[64,144,128]{2,1,0:T(8,128)(2,1)} %send.3), calls=%async_computation.2 | async-start | bytes 4718592 | tf_op jit(solution)/shard_map/all_to_all | solution.py:249
  15.9 0.0 copy-start.4
  15.9 1.5 copy-done.4
  17.4 0.2 halves.1
  17.6 0.1 collective-permute-start
  17.7 1.9 collective-permute-done.refs_1_
  19.6 4.1 %send.2 = bf16[64,176,128]{2,1,0:T(8,128)(2,1)} custom-call(s32[4,128]{1,0:T(4,128)} %bitcast.11, s32[8,128]{1,0:T(8,128)} %bitcast.7, f32[8,128]{1,0:T(8,128)} %bitcast.15, bf16[128,3584]{1,0:T(8,128)(2,1)} %tok_in.3, f32[64,32,128]{2,1,0:T(8,128)S(1)} %get-tuple-element.8.refs_0_, bf16[64,32,128]{2,1,0:T(8,128)(2,1)S(1)} %collective-permute-done.refs_1_), custom_call_target="tpu_custom_call" | custom-call | tf_op jit(solution)/shard_map/send/pallas_call | solution.py:253
  23.6 22.8 %all-to-all-done.2.own_ref = bf16[64,144,128]{2,1,0:T(8,128)(2,1)S(1)} async-done(((bf16[64,144,128]{2,1,0:T(8,128)(2,1)}), bf16[64,144,128]{2,1,0:T(8,128)(2,1)S(1)}, u32[]{:S(2)}, u32[]{:S(2)}) %all-to-all-start.2) | async-done | bytes 2359328 | tf_op jit(solution)/shard_map/all_to_all | solution.py:249
  46.5 0.0 copy-start.2
  46.5 1.4 copy-done.2
  47.9 8.6 %all-to-all-start = ((bf16[64,176,128]{2,1,0:T(8,128)(2,1)}), bf16[64,176,128]{2,1,0:T(8,128)(2,1)S(1)}, u32[]{:S(2)}, u32[]{:S(2)}) async-start(bf16[64,176,128]{2,1,0:T(8,128)(2,1)} %send.2), calls=%async_computation | async-start | bytes 5767168 | tf_op jit(solution)/shard_map/all_to_all | solution.py:249
  56.5 0.1 collective-permute-start.3
  56.6 35.0 %all-to-all-done.own_ref = bf16[64,176,128]{2,1,0:T(8,128)(2,1)S(1)} async-done(((bf16[64,176,128]{2,1,0:T(8,128)(2,1)}), bf16[64,176,128]{2,1,0:T(8,128)(2,1)S(1)}, u32[]{:S(2)}, u32[]{:S(2)}) %all-to-all-start) | async-done | bytes 2883616 | tf_op jit(solution)/shard_map/all_to_all | solution.py:249
  91.6 0.0 copy-start
  91.6 0.0 collective-permute-start.1
  91.6 0.0 collective-permute-done.3.other_ref
  91.6 0.0 copy-start.3
  91.6 2.7 %copy-done.3 = bf16[64,144,128]{2,1,0:T(8,128)(2,1)S(1)} copy-done((bf16[64,144,128]{2,1,0:T(8,128)(2,1)S(1)}, bf16[64,144,128]{2,1,0:T(8,128)(2,1)}, u32[]{:S(2)}) %copy-start.3) | copy-done | bytes 2359320
  94.3 22.7 %experts.3 = (bf16[64,144,128]{2,1,0:T(8,128)(2,1)S(1)}, bf16[64,144,128]{2,1,0:T(8,128)(2,1)S(1)}) custom-call(s32[1]{0:T(128)} %bitcast.2.core_ref, bf16[64,144,128]{2,1,0:T(8,128)(2,1)S(1)} %copy-done.3, bf16[64,144,128]{2,1,0:T(8,128)(2,1)} %collective-permute-done.3.other_ref, bf16[1,3584,1024]{2,1,0:T(8,128)(2,1)} %gate_ref.3, ...), custom_call_target="tpu_custom_call" | custom-call | flops 14092861440 | bytes 40370176 | tf_op jit(solution)/shard_map/experts/pallas_call | solution.py:267
  117.0 0.3 collective-permute-start.4
  117.3 0.0 collective-permute-done.1.other_ref
  117.3 0.0 copy-done
  117.3 0.0 copy-start.5
  117.3 1.6 copy-done.5
  118.9 24.3 %experts.2 = (bf16[64,144,128]{2,1,0:T(8,128)(2,1)S(1)}, bf16[64,144,128]{2,1,0:T(8,128)(2,1)}) custom-call(s32[1]{0:T(128)} %bitcast.2.core_ref, bf16[64,176,128]{2,1,0:T(8,128)(2,1)S(1)} %all-to-all-done.own_ref, bf16[64,176,128]{2,1,0:T(8,128)(2,1)} %copy-done.5, bf16[1,3584,1024]{2,1,0:T(8,128)(2,1)} %gate_ref.3, bf16[1,3584,1024]{2,1,0:T(8,128)(2,1)} %up_ref.3, ...), custom_call_target="tpu_custom_call" | custom-call | flops 14092861440 | bytes 40370176 | tf_op jit(solution)/shard_map/experts/pallas_call | solution.py:267
  143.2 0.0 copy-start.1
  143.2 1.5 copy-done.1
  144.7 0.5 collective-permute-start.2
  145.2 0.0 collective-permute-done.4
  145.2 2.1 add_convert_fusion
  147.3 9.2 %all-to-all-start.3 = ((bf16[64,144,128]{2,1,0:T(8,128)(2,1)}), bf16[64,144,128]{2,1,0:T(8,128)(2,1)S(1)}, u32[]{:S(2)}, u32[]{:S(2)}) async-start(bf16[64,144,128]{2,1,0:T(8,128)(2,1)} %add_convert_fusion), calls=%async_computation.3 | async-start | bytes 4718592 | tf_op jit(solution)/shard_map/all_to_all | solution.py:249
  156.5 0.0 collective-permute-done.2
  156.5 4.4 %add_convert_fusion.1 = bf16[64,144,128]{2,1,0:T(8,128)(2,1)} fusion(bf16[64,144,128]{2,1,0:T(8,128)(2,1)} %collective-permute-done.2, bf16[64,144,128]{2,1,0:T(8,128)(2,1)} %copy-done.1), kind=kLoop, calls=%fused_computation.1 | loop fusion | flops 4718592 | bytes 7077888 | tf_op jit(solution)/shard_map/convert_element_type | solution.py:296
  160.9 26.4 %all-to-all-done.3.msg_in = bf16[64,144,128]{2,1,0:T(8,128)(2,1)S(1)} async-done(((bf16[64,144,128]{2,1,0:T(8,128)(2,1)}), bf16[64,144,128]{2,1,0:T(8,128)(2,1)S(1)}, u32[]{:S(2)}, u32[]{:S(2)}) %all-to-all-start.3) | async-done | bytes 2359328 | tf_op jit(solution)/shard_map/all_to_all | solution.py:249
  187.3 8.9 %all-to-all-start.1 = ((bf16[64,144,128]{2,1,0:T(8,128)(2,1)}), bf16[64,144,128]{2,1,0:T(8,128)(2,1)}, u32[]{:S(2)}, u32[]{:S(2)}) async-start(bf16[64,144,128]{2,1,0:T(8,128)(2,1)} %add_convert_fusion.1), calls=%async_computation.1 | async-start | bytes 4718592 | tf_op jit(solution)/shard_map/all_to_all | solution.py:249
  196.3 1.2 convert_reduce_fusion
  197.5 0.6 slice_select_fusion
  198.1 3.8 %mix.2.refs_0_ = f32[128,3584]{1,0:T(8,128)} custom-call(s32[4,128]{1,0:T(4,128)} %bitcast.12, s32[8,128]{1,0:T(8,128)} %bitcast.8, bf16[64,144,128]{2,1,0:T(8,128)(2,1)S(1)} %all-to-all-done.3.msg_in), custom_call_target="tpu_custom_call" | custom-call | tf_op jit(solution)/shard_map/mix/pallas_call | solution.py:299
  201.9 23.5 %all-to-all-done.1.msg_in = bf16[64,144,128]{2,1,0:T(8,128)(2,1)} async-done(((bf16[64,144,128]{2,1,0:T(8,128)(2,1)}), bf16[64,144,128]{2,1,0:T(8,128)(2,1)}, u32[]{:S(2)}, u32[]{:S(2)}) %all-to-all-start.1) | async-done | bytes 2359328 | tf_op jit(solution)/shard_map/all_to_all | solution.py:249
  225.4 4.2 %mix.3 = bf16[128,3584]{1,0:T(8,128)(2,1)} custom-call(s32[4,128]{1,0:T(4,128)} %bitcast.13, s32[8,128]{1,0:T(8,128)} %bitcast.9, bf16[64,144,128]{2,1,0:T(8,128)(2,1)} %all-to-all-done.1.msg_in, f32[128,3584]{1,0:T(8,128)} %mix.2.refs_0_), custom_call_target="tpu_custom_call" | custom-call | tf_op jit(solution)/shard_map/mix/pallas_call | solution.py:299
  (2 shorter events, 0.0 us)
Async XLA Ops:
  4.5 42.0 %all-to-all-start.2 = ((bf16[64,144,128]{2,1,0:T(8,128)(2,1)}), bf16[64,144,128]{2,1,0:T(8,128)(2,1)S(1)}, u32[]{:S(2)}, u32[]{:S(2)}) async-start(bf16[64,144,128]{2,1,0:T(8,128)(2,1)} %send.3), calls=%async_computation.2 | async-start | bytes 4718592 | tf_op jit(solution)/shard_map/all_to_all | solution.py:249
  15.9 1.5 copy-start.4
  17.6 2.0 collective-permute-start
  46.5 1.4 copy-start.2
  47.9 43.6 %all-to-all-start = ((bf16[64,176,128]{2,1,0:T(8,128)(2,1)}), bf16[64,176,128]{2,1,0:T(8,128)(2,1)S(1)}, u32[]{:S(2)}, u32[]{:S(2)}) async-start(bf16[64,176,128]{2,1,0:T(8,128)(2,1)} %send.2), calls=%async_computation | async-start | bytes 5767168 | tf_op jit(solution)/shard_map/all_to_all | solution.py:249
  56.5 35.1 %collective-permute-start.3 = (bf16[64,144,128]{2,1,0:T(8,128)(2,1)}, bf16[64,144,128]{2,1,0:T(8,128)(2,1)}, u32[]{:S(2)}, u32[]{:S(2)}) collective-permute-start(bf16[64,144,128]{2,1,0:T(8,128)(2,1)} %copy-done.2), channel_id=1, source_target_pairs={{0,1},{1,0},{2,3},{3,2},{4,5},{5,4},{6,7},{7,6},{8,9},{9,8},{10,11... | collective-permute-start | bytes 7077896 | tf_op jit(solution)/shard_map/ppermute | solution.py:293
  91.6 25.8 %copy-start = (bf16[64,176,128]{2,1,0:T(8,128)(2,1)}, bf16[64,176,128]{2,1,0:T(8,128)(2,1)S(1)}, u32[]{:S(2)}) copy-start(bf16[64,176,128]{2,1,0:T(8,128)(2,1)S(1)} %all-to-all-done.own_ref) | copy-start | bytes 8650756
  91.6 25.7 %collective-permute-start.1 = (bf16[64,176,128]{2,1,0:T(8,128)(2,1)S(1)}, bf16[64,176,128]{2,1,0:T(8,128)(2,1)S(1)}, u32[]{:S(2)}, u32[]{:S(2)}) collective-permute-start(bf16[64,176,128]{2,1,0:T(8,128)(2,1)S(1)} %all-to-all-done.own_ref), channel_id=1, source_target_pairs={{0,1},{1,0},{2,3},{3,2},{4,5},{5,4},{6,7},{7,6},{8,9},{9,8},{10,11... | collective-permute-start | bytes 8650760 | tf_op jit(solution)/shard_map/ppermute | solution.py:293
  91.6 2.7 %copy-start.3 = (bf16[64,144,128]{2,1,0:T(8,128)(2,1)S(1)}, bf16[64,144,128]{2,1,0:T(8,128)(2,1)}, u32[]{:S(2)}) copy-start(bf16[64,144,128]{2,1,0:T(8,128)(2,1)} %copy-done.2) | copy-start | bytes 7077892
  117.0 28.1 %collective-permute-start.4 = (bf16[64,144,128]{2,1,0:T(8,128)(2,1)S(1)}, bf16[64,144,128]{2,1,0:T(8,128)(2,1)S(1)}, u32[]{:S(2)}, u32[]{:S(2)}) collective-permute-start(bf16[64,144,128]{2,1,0:T(8,128)(2,1)S(1)} %get-tuple-element.13), channel_id=1, source_target_pairs={{0,1},{1,0},{2,3},{3,2},{4,5},{5,4},{6,7},{7,6},{8,9},{9,8},{10,11... | collective-permute-start | bytes 7077896 | tf_op jit(solution)/shard_map/ppermute | solution.py:295
  117.3 1.6 copy-start.5
  143.2 1.5 copy-start.1
  144.7 11.8 %collective-permute-start.2 = (bf16[64,144,128]{2,1,0:T(8,128)(2,1)}, bf16[64,144,128]{2,1,0:T(8,128)(2,1)}, u32[]{:S(2)}, u32[]{:S(2)}) collective-permute-start(bf16[64,144,128]{2,1,0:T(8,128)(2,1)} %get-tuple-element.11), channel_id=1, source_target_pairs={{0,1},{1,0},{2,3},{3,2},{4,5},{5,4},{6,7},{7,6},{8,9},{9,8},{10,11... | collective-permute-start | bytes 7077896 | tf_op jit(solution)/shard_map/ppermute | solution.py:295
  147.3 40.1 %all-to-all-start.3 = ((bf16[64,144,128]{2,1,0:T(8,128)(2,1)}), bf16[64,144,128]{2,1,0:T(8,128)(2,1)S(1)}, u32[]{:S(2)}, u32[]{:S(2)}) async-start(bf16[64,144,128]{2,1,0:T(8,128)(2,1)} %add_convert_fusion), calls=%async_computation.3 | async-start | bytes 4718592 | tf_op jit(solution)/shard_map/all_to_all | solution.py:249
  187.3 38.1 %all-to-all-start.1 = ((bf16[64,144,128]{2,1,0:T(8,128)(2,1)}), bf16[64,144,128]{2,1,0:T(8,128)(2,1)}, u32[]{:S(2)}, u32[]{:S(2)}) async-start(bf16[64,144,128]{2,1,0:T(8,128)(2,1)} %add_convert_fusion.1), calls=%async_computation.1 | async-start | bytes 4718592 | tf_op jit(solution)/shard_map/all_to_all | solution.py:249

commit v5 on v1

--- a/solution.py
+++ b/solution.py
@@ -194,27 +194,38 @@
 
 
 def fold_kernel(place_ref, *refs):
-    parts, (total_ref, outs) = refs[:-5], (refs[-1], refs[-5:-1])
-    total = parts[0][...].astype(F32)
-    for part in parts[1:]:
-        total = total + part[...].astype(F32)
-    total_ref[...] = total
-    size = total_ref.shape[0] // 4
-    for flip, out_ref in enumerate(outs):
-        at = jnp.bitwise_xor(place_ref[0], flip) * size
-        out_ref[...] = total_ref[pl.ds(at, size)].astype(out_ref.dtype)
-
-
-def mix_kernel(start, node_in, local_in, in_ref, *refs):
-    before, (out_ref, flat_ref, rows_ref, node_ref, local_ref, sum_ref, sem) = refs[:-7], refs[-7:]
-    copies = load_all([(node_in, node_ref), (local_in, local_ref)] + [(old, sum_ref) for old in before], sem)
+    parts, (outs, stages, sem) = refs[:-9], (refs[-9:-5], refs[-5:-1], refs[-1])
+    size = outs[0].shape[0]
+    saves = []
+    for flip in range(4):
+        at = pl.ds(jnp.bitwise_xor(place_ref[0], flip) * size, size)
+        total = parts[0][at].astype(F32)
+        for part in parts[1:]:
+            total = total + part[at].astype(F32)
+        stages[flip][...] = total.astype(stages[flip].dtype)
+        saves.append(pltpu.make_async_copy(stages[flip], outs[flip], sem.at[flip]))
+        saves[-1].start()
+    for save in saves:
+        save.wait()
+
+
+def mix_kernel(start, node_in, local_in, msg_in, *refs):
+    before, (out_ref, flat_ref, rows_ref, node_ref, local_ref, msg_ref, sum_ref, sem) = refs[:-8], refs[-8:]
+    loads = [(node_in, node_ref), (local_in, local_ref)]
+    if before:
+        loads += [(msg_in.at[cut], msg_ref.at[cut]) for cut in CUTS] + [(before[0], sum_ref)]
+    copies = load_all(loads, sem)
     copies[0].wait()
     copies[1].wait()
     pick = jnp.concatenate(picks(node_ref, local_ref, start), axis=0).astype(BF16)
-    spread(in_ref, flat_ref)
+    for i, cut in enumerate(CUTS):
+        if before:
+            copies[2 + i].wait()
+        arrived = msg_ref[cut] if before else msg_in[cut]
+        flat_ref.reshape(PAIRS, PITCH, 128)[cut, :MSG, :] = arrived.astype(F32)
     lay_out(flat_ref, rows_ref, 0, WIDE)
-    for copy in copies[2:]:
-        copy.wait()
+    if before:
+        copies[-1].wait()
     for k in range(7):
         at = slice(512 * k, 512 * (k + 1))
         value = lax.dot_general(pick, rows_ref[:, at], (((0,), (0,)), ((), ())), preferred_element_type=F32)
@@ -299,14 +310,14 @@
         return (mine.astype(F32) + back.astype(F32)).astype(BF16)
 
     def fold(axes, dtype, *parts):
-        size = parts[0].shape[0] // 4
-        shapes = [jax.ShapeDtypeStruct((size, GRAD, 128), F32)] + [jax.ShapeDtypeStruct((size, GRAD, 128), dtype)] * 3
+        shape = (parts[0].shape[0] // 4, GRAD, 128)
+        kinds = (F32, dtype, dtype, dtype)
         kept, *given = pl.pallas_call(
             fold_kernel,
             in_specs=[scalar] + [local] * len(parts),
-            out_specs=[local] * 4,
-            out_shape=shapes,
-            scratch_shapes=[pltpu.VMEM(parts[0].shape, F32)],
+            out_specs=[far] * 4,
+            out_shape=[pltpu.HBM(shape, kind) for kind in kinds],
+            scratch_shapes=[pltpu.VMEM(shape, kind) for kind in kinds] + [dma((4,))],
             compiler_params=vmem(16),
             name="fold",
         )(place(axes), *parts)
@@ -317,14 +328,14 @@
     def mix(start, message, *before):
         return pl.pallas_call(
             functools.partial(mix_kernel, start),
-            in_specs=[far, far, local] + [far] * len(before),
+            in_specs=[far, far] + ([far, far] if before else [local]),
             out_shape=jax.ShapeDtypeStruct((tok, width), BF16) if before else pltpu.HBM((tok, width), F32),
             scratch_shapes=[flat, rows]
             + small
-            + [pltpu.VMEM((tok, width), F32), dma((3,))],
+            + [pltpu.VMEM((PAIRS, MSG, 128), BF16), pltpu.VMEM((tok, width), F32), dma((7,))],
             compiler_params=vmem(32),
             name="mix",
-        )(*map(in_hbm, routes), message, *map(in_hbm, before))
+        )(*map(in_hbm, routes), in_hbm(message) if before else message, *map(in_hbm, before))
 
     halves = pl.pallas_call(
         halves_kernel,

time: 256 us -> 258 us (level)
  transfers between devices with their start and end apart: 16 -> 16, of which waited for: 10 -> 11; matrix products, arithmetic and copies ran while one was open for 3% -> 3% of each run, Pallas kernels for 22% -> 22%
where the time goes in v5:
time: 258 us; the launch traced here: 255 us
  blocking collectives  82 us (32%)
  Pallas kernels  67.7 us (26%)
  waiting for transfers between devices  61.4 us (24%)
  starting transfers between devices  30 us (12%)
  other arithmetic  7.87 us (3%)
  local copies, waits for them, and re-layouts  4.78 us (2%)
    all_to_all x2, blocking collectives, exchange(): lax.all_to_all(message, chips, split_axis=0, concat_axis=0, tiled=True)  82 us
    pallas_call x2, Pallas kernels, experts(): pl.pallas_call(expert_kernel, in_specs=[scalar, local, local] + [far] * 3...  47.6 us
    ppermute x9, waiting for transfers between devices, fold(): lax.ppermute(part, axes, [(i, i ^ flip) for i in range(4)])  32.1 us
    all_to_all x2, waiting for transfers between devices, exchange(): lax.all_to_all(message, chips, split_axis=0, concat_axis=0, tiled=True)  27 us
    all_to_all x2, starting transfers between devices, exchange(): lax.all_to_all(message, chips, split_axis=0, concat_axis=0, tiled=True)  17.4 us
    ppermute x9, starting transfers between devices, fold(): lax.ppermute(part, axes, [(i, i ^ flip) for i in range(4)])  11.9 us
    pallas_call x2, Pallas kernels, mix(): pl.pallas_call(functools.partial(mix_kernel, start), in_specs=[far, far]...  8.15 us
    pallas_call x2, Pallas kernels, send(): pl.pallas_call(functools.partial(send_kernel, start), in_specs=[far] * 4,...  7.72 us
  transfers between devices with their start and end apart: 16, of which 11 were waited for; matrix products, arithmetic and copies ran while one was open for 3% of the time, Pallas kernels for 22%

profile of v5, /device:TPU:10, one launch (start us, length us, event | category | flops | bytes accessed | tf_op | source)
XLA Modules:
  0.0 254.8 jit_solution(6661995405783130618)
XLA Ops:
  0.6 3.9 %send.3 = bf16[64,144,128]{2,1,0:T(8,128)(2,1)} custom-call(s32[4,128]{1,0:T(4,128)} %bitcast.21, s32[8,128]{1,0:T(8,128)} %bitcast.17, f32[8,128]{1,0:T(8,128)} %bitcast.25, bf16[128,3584]{1,0:T(8,128)(2,1)} %tok_in.3), custom_call_target="tpu_custom_call" | custom-call | tf_op jit(solution)/shard_map/send/pallas_call | solution.py:267
  4.5 42.5 %all_to_all.20.own_ref = bf16[64,144,128]{2,1,0:T(8,128)(2,1)S(1)} all-to-all(bf16[64,144,128]{2,1,0:T(8,128)(2,1)} %send.3), channel_id=1, replica_groups=mesh['edp'=2,'zh'=2,'x'=4,'y'=4,'core'=2] {'edp','zh','x','y'}, dimensions={0} | all-to-all | bytes 4718592 | tf_op jit(solution)/shard_map/all_to_all | solution.py:263
  47.0 0.0 collective-permute-start.2
  47.0 3.9 %send.2 = bf16[64,144,128]{2,1,0:T(8,128)(2,1)} custom-call(s32[4,128]{1,0:T(4,128)} %bitcast.22, s32[8,128]{1,0:T(8,128)} %bitcast.18, f32[8,128]{1,0:T(8,128)} %bitcast.26, bf16[128,3584]{1,0:T(8,128)(2,1)} %tok_in.3), custom_call_target="tpu_custom_call" | custom-call | tf_op jit(solution)/shard_map/send/pallas_call | solution.py:267
  50.9 39.5 %all_to_all.21.own_ref = bf16[64,144,128]{2,1,0:T(8,128)(2,1)} all-to-all(bf16[64,144,128]{2,1,0:T(8,128)(2,1)} %send.2), channel_id=1, replica_groups=mesh['edp'=2,'zh'=2,'x'=4,'y'=4,'core'=2] {'edp','zh','x','y'}, dimensions={0} | all-to-all | bytes 4718592 | tf_op jit(solution)/shard_map/all_to_all | solution.py:263
  90.4 0.0 collective-permute-start
  90.4 0.0 collective-permute-done.2.other_ref
  90.4 22.7 %experts.3 = (bf16[64,144,128]{2,1,0:T(8,128)(2,1)S(1)}, bf16[64,144,128]{2,1,0:T(8,128)(2,1)S(1)}) custom-call(s32[1]{0:T(128)} %bitcast.2.core_ref, bf16[64,144,128]{2,1,0:T(8,128)(2,1)S(1)} %all_to_all.20.own_ref, bf16[64,144,128]{2,1,0:T(8,128)(2,1)} %collective-permute-done.2.other_ref, bf16[1,3584,1024]{2,1,0:T(8,128)(2,1)} %gate_ref.3, ...), custom_call_target="tpu_custom_call" | custom-call | flops 14092861440 | bytes 40370176 | tf_op jit(solution)/shard_map/experts/pallas_call | solution.py:281
  113.2 0.8 collective-permute-start.3
  113.9 0.0 collective-permute-done.other_ref
  113.9 24.8 %experts.2 = (bf16[64,144,128]{2,1,0:T(8,128)(2,1)S(1)}, bf16[64,144,128]{2,1,0:T(8,128)(2,1)}) custom-call(s32[1]{0:T(128)} %bitcast.2.core_ref, bf16[64,144,128]{2,1,0:T(8,128)(2,1)} %all_to_all.21.own_ref, bf16[64,144,128]{2,1,0:T(8,128)(2,1)} %collective-permute-done.other_ref, bf16[1,3584,1024]{2,1,0:T(8,128)(2,1)} %gate_ref.3, ...), custom_call_target="tpu_custom_call" | custom-call | flops 14092861440 | bytes 40370176 | tf_op jit(solution)/shard_map/experts/pallas_call | solution.py:281
  138.8 0.0 copy-start
  138.8 1.5 copy-done
  140.2 0.0 collective-permute-start.1
  140.3 0.0 collective-permute-done.3
  140.3 2.1 add_convert_fusion
  142.4 7.9 %all-to-all-start.3 = ((bf16[64,144,128]{2,1,0:T(8,128)(2,1)}), bf16[64,144,128]{2,1,0:T(8,128)(2,1)S(1)}, u32[]{:S(2)}, u32[]{:S(2)}) async-start(bf16[64,144,128]{2,1,0:T(8,128)(2,1)} %add_convert_fusion), calls=%async_computation.3 | async-start | bytes 4718592 | tf_op jit(solution)/shard_map/all_to_all | solution.py:263
  150.3 0.0 collective-permute-done.1
  150.3 4.4 %add_convert_fusion.1 = bf16[64,144,128]{2,1,0:T(8,128)(2,1)} fusion(bf16[64,144,128]{2,1,0:T(8,128)(2,1)} %collective-permute-done.1, bf16[64,144,128]{2,1,0:T(8,128)(2,1)} %copy-done), kind=kLoop, calls=%fused_computation.1 | loop fusion | flops 4718592 | bytes 7077888 | tf_op jit(solution)/shard_map/convert_element_type | solution.py:310
  154.8 27.0 %all-to-all-done.3.msg_in = bf16[64,144,128]{2,1,0:T(8,128)(2,1)S(1)} async-done(((bf16[64,144,128]{2,1,0:T(8,128)(2,1)}), bf16[64,144,128]{2,1,0:T(8,128)(2,1)S(1)}, u32[]{:S(2)}, u32[]{:S(2)}) %all-to-all-start.3) | async-done | bytes 2359328 | tf_op jit(solution)/shard_map/all_to_all | solution.py:263
  181.8 9.4 %all-to-all-start.1 = ((bf16[64,144,128]{2,1,0:T(8,128)(2,1)}), bf16[64,144,128]{2,1,0:T(8,128)(2,1)}, u32[]{:S(2)}, u32[]{:S(2)}) async-start(bf16[64,144,128]{2,1,0:T(8,128)(2,1)} %add_convert_fusion.1), calls=%async_computation.1 | async-start | bytes 4718592 | tf_op jit(solution)/shard_map/all_to_all | solution.py:263
  191.2 0.0 copy-start.1
  191.3 1.5 copy-done.1
  192.7 1.0 halves.1
  193.7 0.0 collective-permute-start.4
  193.7 2.2 collective-permute-done.4.refs_1_
  196.0 1.9 fold.3
  197.9 3.1 %collective-permute-start.5 = (bf16[16,32,128]{2,1,0:T(8,128)(2,1)}, bf16[16,32,128]{2,1,0:T(8,128)(2,1)S(1)}, u32[]{:S(2)}, u32[]{:S(2)}) collective-permute-start(bf16[16,32,128]{2,1,0:T(8,128)(2,1)} %get-tuple-element.27), channel_id=1, source_target_pairs={{0,32},{32,0},{64,96},{96,64},{1,33},{33,1},{65,97},{97,65},{2,34}... | collective-permute-start | bytes 393224 | tf_op jit(solution)/shard_map/ppermute | solution.py:325
  201.0 0.8 collective-permute-start.6
  201.8 0.5 collective-permute-start.7
  202.3 21.5 %collective-permute-done.5.refs_1_ = bf16[16,32,128]{2,1,0:T(8,128)(2,1)S(1)} collective-permute-done((bf16[16,32,128]{2,1,0:T(8,128)(2,1)}, bf16[16,32,128]{2,1,0:T(8,128)(2,1)S(1)}, u32[]{:S(2)}, u32[]{:S(2)}) %collective-permute-start.5) | collective-permute-done | bytes 131104 | tf_op jit(solution)/shard_map/ppermute | solution.py:325
  223.7 0.3 collective-permute-done.6.refs_2_
  224.0 0.6 collective-permute-done.7.refs_3_
  224.6 0.0 copy-start.2
  224.6 0.9 copy-done.2
  225.6 0.7 fold.4
  226.3 1.8 collective-permute-start.10
  228.2 1.5 collective-permute-start.8
  229.7 0.2 collective-permute-start.9
  229.9 1.0 collective-permute-done.10.refs_3_
  230.9 2.4 collective-permute-done.8.refs_1_
  233.2 2.4 collective-permute-done.9.refs_2_
  235.7 0.0 copy-start.3
  235.7 0.8 copy-done.3
  236.5 0.7 fold.5
  237.2 1.6 collective-permute-start.11
  238.8 2.4 collective-permute-start.12
  241.1 0.0 collective-permute-start.13
  241.1 0.1 collective-permute-done.11
  241.2 3.0 %collective-permute-done.12 = f32[1,32,128]{2,1,0:T(8,128)S(1)} collective-permute-done((f32[1,32,128]{2,1,0:T(8,128)}, f32[1,32,128]{2,1,0:T(8,128)S(1)}, u32[]{:S(2)}, u32[]{:S(2)}) %collective-permute-start.12) | collective-permute-done | bytes 16416 | tf_op jit(solution)/shard_map/ppermute | solution.py:325
  244.2 0.8 collective-permute-done.13
  245.1 0.7 add_add_fusion
  245.8 0.6 fusion
  246.4 3.9 %mix.2.refs_0_ = f32[128,3584]{1,0:T(8,128)} custom-call(s32[4,128]{1,0:T(4,128)} %bitcast.23, s32[8,128]{1,0:T(8,128)} %bitcast.19, bf16[64,144,128]{2,1,0:T(8,128)(2,1)S(1)} %all-to-all-done.3.msg_in), custom_call_target="tpu_custom_call" | custom-call | tf_op jit(solution)/shard_map/mix/pallas_call | solution.py:329
  250.3 0.0 all-to-all-done.1.msg_in
  250.3 4.2 %mix.3 = bf16[128,3584]{1,0:T(8,128)(2,1)} custom-call(s32[4,128]{1,0:T(4,128)} %bitcast.24, s32[8,128]{1,0:T(8,128)} %bitcast.20, bf16[64,144,128]{2,1,0:T(8,128)(2,1)} %all-to-all-done.1.msg_in, f32[128,3584]{1,0:T(8,128)} %mix.2.refs_0_), custom_call_target="tpu_custom_call" | custom-call | tf_op jit(solution)/shard_map/mix/pallas_call | solution.py:329
  (2 shorter events, 0.0 us)
Async XLA Ops:
  47.0 43.4 %collective-permute-start.2 = (bf16[64,144,128]{2,1,0:T(8,128)(2,1)S(1)}, bf16[64,144,128]{2,1,0:T(8,128)(2,1)}, u32[]{:S(2)}, u32[]{:S(2)}) collective-permute-start(bf16[64,144,128]{2,1,0:T(8,128)(2,1)S(1)} %all_to_all.20.own_ref), channel_id=1, source_target_pairs={{0,1},{1,0},{2,3},{3,2},{4,5},{5,4},{6,7},{7,6},{8,9},{9,8},{10,11... | collective-permute-start | bytes 7077896 | tf_op jit(solution)/shard_map/ppermute | solution.py:307
  90.4 23.5 %collective-permute-start = (bf16[64,144,128]{2,1,0:T(8,128)(2,1)}, bf16[64,144,128]{2,1,0:T(8,128)(2,1)}, u32[]{:S(2)}, u32[]{:S(2)}) collective-permute-start(bf16[64,144,128]{2,1,0:T(8,128)(2,1)} %all_to_all.21.own_ref), channel_id=1, source_target_pairs={{0,1},{1,0},{2,3},{3,2},{4,5},{5,4},{6,7},{7,6},{8,9},{9,8},{10,11... | collective-permute-start | bytes 7077896 | tf_op jit(solution)/shard_map/ppermute | solution.py:307
  113.2 27.1 %collective-permute-start.3 = (bf16[64,144,128]{2,1,0:T(8,128)(2,1)S(1)}, bf16[64,144,128]{2,1,0:T(8,128)(2,1)S(1)}, u32[]{:S(2)}, u32[]{:S(2)}) collective-permute-start(bf16[64,144,128]{2,1,0:T(8,128)(2,1)S(1)} %get-tuple-element.23), channel_id=1, source_target_pairs={{0,1},{1,0},{2,3},{3,2},{4,5},{5,4},{6,7},{7,6},{8,9},{9,8},{10,11... | collective-permute-start | bytes 7077896 | tf_op jit(solution)/shard_map/ppermute | solution.py:309
  138.8 1.5 copy-start
  140.2 10.1 %collective-permute-start.1 = (bf16[64,144,128]{2,1,0:T(8,128)(2,1)}, bf16[64,144,128]{2,1,0:T(8,128)(2,1)}, u32[]{:S(2)}, u32[]{:S(2)}) collective-permute-start(bf16[64,144,128]{2,1,0:T(8,128)(2,1)} %get-tuple-element.21), channel_id=1, source_target_pairs={{0,1},{1,0},{2,3},{3,2},{4,5},{5,4},{6,7},{7,6},{8,9},{9,8},{10,11... | collective-permute-start | bytes 7077896 | tf_op jit(solution)/shard_map/ppermute | solution.py:309
  142.4 39.4 %all-to-all-start.3 = ((bf16[64,144,128]{2,1,0:T(8,128)(2,1)}), bf16[64,144,128]{2,1,0:T(8,128)(2,1)S(1)}, u32[]{:S(2)}, u32[]{:S(2)}) async-start(bf16[64,144,128]{2,1,0:T(8,128)(2,1)} %add_convert_fusion), calls=%async_computation.3 | async-start | bytes 4718592 | tf_op jit(solution)/shard_map/all_to_all | solution.py:263
  181.8 68.5 %all-to-all-start.1 = ((bf16[64,144,128]{2,1,0:T(8,128)(2,1)}), bf16[64,144,128]{2,1,0:T(8,128)(2,1)}, u32[]{:S(2)}, u32[]{:S(2)}) async-start(bf16[64,144,128]{2,1,0:T(8,128)(2,1)} %add_convert_fusion.1), calls=%async_computation.1 | async-start | bytes 4718592 | tf_op jit(solution)/shard_map/all_to_all | solution.py:263
  191.2 1.5 copy-start.1
  193.7 2.3 collective-permute-start.4
  197.9 25.8 %collective-permute-start.5 = (bf16[16,32,128]{2,1,0:T(8,128)(2,1)}, bf16[16,32,128]{2,1,0:T(8,128)(2,1)S(1)}, u32[]{:S(2)}, u32[]{:S(2)}) collective-permute-start(bf16[16,32,128]{2,1,0:T(8,128)(2,1)} %get-tuple-element.27), channel_id=1, source_target_pairs={{0,32},{32,0},{64,96},{96,64},{1,33},{33,1},{65,97},{97,65},{2,34}... | collective-permute-start | bytes 393224 | tf_op jit(solution)/shard_map/ppermute | solution.py:325
  201.0 23.1 %collective-permute-start.6 = (bf16[16,32,128]{2,1,0:T(8,128)(2,1)}, bf16[16,32,128]{2,1,0:T(8,128)(2,1)S(1)}, u32[]{:S(2)}, u32[]{:S(2)}) collective-permute-start(bf16[16,32,128]{2,1,0:T(8,128)(2,1)} %get-tuple-element.28), channel_id=1, source_target_pairs={{0,64},{32,96},{64,0},{96,32},{1,65},{33,97},{65,1},{97,33},{2,66}... | collective-permute-start | bytes 393224 | tf_op jit(solution)/shard_map/ppermute | solution.py:325
  201.8 22.9 %collective-permute-start.7 = (bf16[16,32,128]{2,1,0:T(8,128)(2,1)}, bf16[16,32,128]{2,1,0:T(8,128)(2,1)S(1)}, u32[]{:S(2)}, u32[]{:S(2)}) collective-permute-start(bf16[16,32,128]{2,1,0:T(8,128)(2,1)} %get-tuple-element.29), channel_id=1, source_target_pairs={{0,96},{32,64},{64,32},{96,0},{1,97},{33,65},{65,33},{97,1},{2,98}... | collective-permute-start | bytes 393224 | tf_op jit(solution)/shard_map/ppermute | solution.py:325
  224.6 1.0 copy-start.2
  226.3 4.6 %collective-permute-start.10 = (f32[4,32,128]{2,1,0:T(8,128)}, f32[4,32,128]{2,1,0:T(8,128)S(1)}, u32[]{:S(2)}, u32[]{:S(2)}) collective-permute-start(f32[4,32,128]{2,1,0:T(8,128)} %get-tuple-element.33), channel_id=1, source_target_pairs={{0,24},{8,16},{16,8},{24,0},{1,25},{9,17},{17,9},{25,1},{2,26},{10... | collective-permute-start | bytes 196616 | tf_op jit(solution)/shard_map/ppermute | solution.py:325
  228.2 5.1 %collective-permute-start.8 = (f32[4,32,128]{2,1,0:T(8,128)}, f32[4,32,128]{2,1,0:T(8,128)S(1)}, u32[]{:S(2)}, u32[]{:S(2)}) collective-permute-start(f32[4,32,128]{2,1,0:T(8,128)} %get-tuple-element.31), channel_id=1, source_target_pairs={{0,8},{8,0},{16,24},{24,16},{1,9},{9,1},{17,25},{25,17},{2,10},{10... | collective-permute-start | bytes 196616 | tf_op jit(solution)/shard_map/ppermute | solution.py:325
  229.7 6.0 %collective-permute-start.9 = (f32[4,32,128]{2,1,0:T(8,128)}, f32[4,32,128]{2,1,0:T(8,128)S(1)}, u32[]{:S(2)}, u32[]{:S(2)}) collective-permute-start(f32[4,32,128]{2,1,0:T(8,128)} %get-tuple-element.32), channel_id=1, source_target_pairs={{0,16},{8,24},{16,0},{24,8},{1,17},{9,25},{17,1},{25,9},{2,18},{10... | collective-permute-start | bytes 196616 | tf_op jit(solution)/shard_map/ppermute | solution.py:325
  235.7 0.8 copy-start.3
  237.2 4.0 %collective-permute-start.11 = (f32[1,32,128]{2,1,0:T(8,128)}, f32[1,32,128]{2,1,0:T(8,128)S(1)}, u32[]{:S(2)}, u32[]{:S(2)}) collective-permute-start(f32[1,32,128]{2,1,0:T(8,128)} %get-tuple-element.35), channel_id=1, source_target_pairs={{0,2},{2,0},{4,6},{6,4},{1,3},{3,1},{5,7},{7,5},{8,10},{10,8},{12,... | collective-permute-start | bytes 49160 | tf_op jit(solution)/shard_map/ppermute | solution.py:325
  238.8 5.5 %collective-permute-start.12 = (f32[1,32,128]{2,1,0:T(8,128)}, f32[1,32,128]{2,1,0:T(8,128)S(1)}, u32[]{:S(2)}, u32[]{:S(2)}) collective-permute-start(f32[1,32,128]{2,1,0:T(8,128)} %get-tuple-element.36), channel_id=1, source_target_pairs={{0,4},{2,6},{4,0},{6,2},{1,5},{3,7},{5,1},{7,3},{8,12},{10,14},{12... | collective-permute-start | bytes 49160 | tf_op jit(solution)/shard_map/ppermute | solution.py:325
  241.1 3.9 %collective-permute-start.13 = (f32[1,32,128]{2,1,0:T(8,128)}, f32[1,32,128]{2,1,0:T(8,128)S(1)}, u32[]{:S(2)}, u32[]{:S(2)}) collective-permute-start(f32[1,32,128]{2,1,0:T(8,128)} %get-tuple-element.37), channel_id=1, source_target_pairs={{0,6},{2,4},{4,2},{6,0},{1,7},{3,5},{5,3},{7,1},{8,14},{10,12},{12... | collective-permute-start | bytes 49160 | tf_op jit(solution)/shard_map/ppermute | solution.py:325
